TPU v7x, 128 devices: a whole 4x4x4 slice. The times are simulated.
128 devices in a mesh: grp: 16 (over x_lo, z, core), rep: 8 (over y, x_hi).
Axes of the slice: x: 4 (x_hi: 2, x_lo: 2; x = x_hi * 2 + x_lo), y: 4, z: 4, core: 2. Of those that a mesh axis runs over, the one named last changes fastest.
Arguments:
- queries: bfloat16 [49152, 2560], P(('grp', 'rep')), may hold values from -60 to 60
- passages: bfloat16 [262144, 2560], P(('grp', 'rep')), may hold values from -60 to 60
- block_valid_counts: int32 [2048], P(('grp', 'rep')), may hold values from 16 to 128
- positive_index: int32 [49152], P(('grp', 'rep')), may hold values from 0 to 2047, as said below
- neg_blocks: int32 [128, 28], P(('grp', 'rep')), may hold values from 0 to 2047, as said below
- query_weights: float32 [49152], P(('grp', 'rep')), may hold values from 0.3 to 10
Outputs:
- query_loss: float32 [49152], P(('grp', 'rep'))
- mean_loss: float32 [], replicated
Inputs may be any that keep to these rules, and one draw needn't show every extreme that they name: `neg_blocks`: row g lists 28 distinct blocks, all owned by query groups with the same rep index as group g and another grp index; at most 2 of them belong to one group, and some group gives exactly 2 in every row. `positive_index`: always a valid row of one of the query's own group's blocks.
All inputs are finite; a program needn't handle non-finite values.
Results may differ from a plain program's by a relative error of at most 0.0003.
Values may be sent and summed in bfloat16 or wider, within the bound.
No kernel may reach another device: no remote copies, remote signals or barrier semaphores. Data moves between devices by JAX's collectives and lax.ppermute only.
A program may use at most 256 MiB of HBM per device.

v0:
```python
import jax
import jax.numpy as jnp
from jax import lax
from jax.sharding import Mesh
from jax.sharding import PartitionSpec as P

CAP = 2
GRP = ("grp_0", "grp_1", "grp_2")
REP = ("rep_0", "rep_1")
GRP_REP = ("grp_0", "grp_1", "grp_2", "rep_0", "rep_1")


inverse_softmax_sharpness = 20.0
norm_epsilon = 1e-06


def grouped_exchange(shard, axis, split_dim, concat_dim, work, item_dim, out_dim):
    items = jax.tree.leaves(shard)[0].shape[item_dim]
    count = 2 if items % 2 == 0 else 1
    done = []
    for k in range(count):
        group = jax.tree.map(
            lambda a: lax.slice_in_dim(
                a, k * (items // count), (k + 1) * (items // count), axis=item_dim
            ),
            shard,
        )
        done.append(
            work(
                lax.all_to_all(
                    group, axis, split_axis=split_dim, concat_axis=concat_dim, tiled=True
                )
            )
        )
    return jax.tree.map(lambda *parts: jnp.concatenate(parts, axis=out_dim), *done)


def by_axis(shard, axes):
    for axis in axes:
        shard = lax.psum(shard, axis)
    return shard


def normalize(rows):
    values = rows.astype(jnp.float32)
    scale = lax.rsqrt(jnp.sum(values * values, axis=-1, keepdims=True) + norm_epsilon)
    return (values * scale).astype(jnp.bfloat16)


def local(queries, passages, block_valid_counts, positive_index, neg_blocks, query_weights):
    group_count = lax.axis_size(GRP)
    replica_count = lax.axis_size(REP)
    local_rows = passages.shape[0]
    blocks_here = block_valid_counts.shape[0]
    block_rows = local_rows // blocks_here
    feature_width = passages.shape[1]
    question_unit_vectors = normalize(queries)
    document_unit_vectors = normalize(passages)
    row_valid = jnp.arange(local_rows, dtype=jnp.int32) % block_rows < jnp.repeat(
        block_valid_counts, block_rows
    )
    shared_pool_similarity = (
        lax.dot_general(
            question_unit_vectors,
            document_unit_vectors,
            (((1,), (1,)), ((), ())),
            preferred_element_type=jnp.float32,
        )
        * inverse_softmax_sharpness
    )
    local_total = jnp.sum(
        jnp.where(row_valid[None, :], jnp.exp(shared_pool_similarity), 0.0), axis=1
    )
    positive_score = jnp.take_along_axis(shared_pool_similarity, positive_index[:, None], axis=1)[
        :, 0
    ]
    wanted = neg_blocks[0]
    owner_device = wanted // blocks_here
    owner_group = owner_device // replica_count
    local_block = wanted % blocks_here
    listed = wanted.shape[0]
    same_owner = owner_group[:, None] == owner_group[None, :]
    earlier_slot = jnp.arange(listed)[:, None] > jnp.arange(listed)[None, :]
    slot_rank = jnp.sum(jnp.logical_and(same_owner, earlier_slot), axis=1)
    requests = (
        jnp.full((group_count, CAP), -1, jnp.int32).at[owner_group, slot_rank].set(local_block)
    )
    incoming = lax.all_to_all(requests, GRP, split_axis=0, concat_axis=0, tiled=True)
    requested = incoming >= 0
    safe_block = jnp.maximum(incoming, 0)
    matches = safe_block[:, :, None] == jnp.arange(blocks_here, dtype=jnp.int32)[None, None, :]
    slot_counts = jnp.where(
        requested, jnp.sum(jnp.where(matches, block_valid_counts[None, None, :], 0), axis=2), 0
    )
    unit_blocks = document_unit_vectors.reshape(blocks_here, block_rows, feature_width)
    picked = unit_blocks[safe_block]

    def score_blocks(pair):
        arrived, kept_counts = pair
        similarity = (
            jnp.einsum(
                "qd,skrd->kqsr", question_unit_vectors, arrived, preferred_element_type=jnp.float32
            )
            * inverse_softmax_sharpness
        )
        live_rows = jnp.arange(block_rows, dtype=jnp.int32)[None, None, :] < kept_counts[:, :, None]
        live_rows = jnp.transpose(live_rows, (1, 0, 2))[:, None]
        return jnp.sum(jnp.where(live_rows, jnp.exp(similarity), 0.0), axis=(2, 3))

    slot_totals = grouped_exchange((picked, slot_counts), GRP, 0, 0, score_blocks, 1, 0)
    hard_total = jnp.sum(slot_totals, axis=0)
    query_loss = jnp.log(local_total + hard_total) - positive_score
    weighted_sum, weight_sum = (
        by_axis(jnp.sum(query_weights * query_loss), GRP_REP),
        by_axis(jnp.sum(query_weights), GRP_REP),
    )
    return (query_loss, weighted_sum / weight_sum)


def solution(mesh):
    split = Mesh(mesh.devices.reshape(2, 4, 2, 4, 2), ("grp_0", "grp_1", "grp_2", "rep_0", "rep_1"))
    in_specs = (
        P(GRP_REP, None),
        P(GRP_REP, None),
        P(GRP_REP),
        P(GRP_REP),
        P(GRP_REP, None),
        P(GRP_REP),
    )
    out_specs = (P(GRP_REP), P())
    return jax.shard_map(local, mesh=split, in_specs=in_specs, out_specs=out_specs, check_vma=False)
```

profile of v0, /device:TPU:0, one launch (start us, length us, event | category | flops | bytes accessed | tf_op | source)
XLA Modules:
  0.0 407.0 jit_solution(8738619450794840905)
XLA Ops:
  0.6 0.7 fusion.30
  1.3 0.7 and_select_fusion
  2.0 0.2 convert_reduce_fusion
  2.2 0.7 fusion.31
  2.8 2.0 scatter_fusion
  4.9 0.7 copy.31
  5.6 6.5 %all-to-all-start = ((s32[16,1,2]{2,1,0:T(1,128)}), s32[16,1,2]{2,1,0:T(1,128)S(1)}, u32[]{:S(2)}, u32[]{:S(2)}) async-start(s32[16,1,2]{2,1,0:T(1,128)} %copy.31), calls=%async_computation | async-start | bytes 16384 | tf_op jit(solution)/shard_map/all_to_all | solution.py:88
  12.0 0.0 copy-start
  12.0 6.2 %fusion = f32[2048]{0:T(1024)S(1)} fusion(bf16[2048,2560]{1,0:T(8,128)(2,1)} %param.7), kind=kLoop, calls=%fused_computation.5 | loop fusion | flops 15726592 | bytes 10493952 | tf_op jit(solution)/shard_map/reduce_sum | solution.py:46
  18.3 0.7 copy-done
  19.0 0.0 copy-start.4
  19.0 5.5 %fusion.1 = bf16[2048,2560]{1,0:T(8,128)(2,1)} fusion(bf16[2048,2560]{1,0:T(8,128)(2,1)S(1)} %copy-done, f32[2048]{0:T(1024)S(1)} %add_rsqrt_fusion), kind=kLoop, calls=%fused_computation.6 | loop fusion | flops 15728640 | bytes 20979712 | tf_op jit(solution)/shard_map/convert_element_type | solution.py:47
  24.5 0.0 all-to-all-done
  24.5 0.1 copy.32
  24.6 0.0 copy-done.4
  24.6 0.2 select_reduce_fusion.1
  24.8 0.7 copy.34
  25.5 5.7 %all-to-all-start.1 = ((s32[16,1,1]{2,1,0:T(1,128)}), s32[16,1,1]{2,1,0:T(1,128)S(1)}, u32[]{:S(2)}, u32[]{:S(2)}) async-start(s32[16,1,1]{2,1,0:T(1,128)} %copy.34), calls=%async_computation.1 | async-start | bytes 16384 | tf_op jit(solution)/shard_map/all_to_all | solution.py:30
  31.2 0.1 copy.35
  31.3 0.1 reshape.308
  31.4 0.7 copy.36
  32.0 12.6 %gather_fusion = bf16[32,128,2560]{2,1,0:T(8,128)(2,1)} fusion(bf16[16,128,2560]{2,1,0:T(8,128)(2,1)} %bitcast.83, s32[1024]{0:T(1024)S(1)} %pad_clamp_fusion), kind=kCustom, calls=%fused_computation | custom fusion | bytes 41943168 | tf_op jit(solution)/shard_map/gather | solution.py:96
  44.7 0.0 all-to-all-done.1
  44.7 5.8 %all-to-all-start.3 = ((s32[16,1,1]{2,1,0:T(1,128)}), s32[16,1,1]{2,1,0:T(1,128)S(1)}, u32[]{:S(2)}, u32[]{:S(2)}) async-start(s32[16,1,1]{2,1,0:T(1,128)} %copy.36), calls=%async_computation.3 | async-start | bytes 16384 | tf_op jit(solution)/shard_map/all_to_all | solution.py:30
  50.5 16.3 %fusion.37 = (bf16[16,1,128,2560]{3,2,1,0:T(8,128)(2,1)}, bf16[16,1,128,2560]{3,2,1,0:T(8,128)(2,1)}) fusion(bf16[16,2,128,2560]{3,2,1,0:T(8,128)(2,1)} %bitcast.84), kind=kLoop, calls=%fused_computation.90 | loop fusion | bytes 41943040 | tf_op jit(solution)/shard_map/slice | solution.py:23
  66.8 0.0 all-to-all-done.3
  66.8 123.4 %all_to_all.37 = bf16[16,1,128,2560]{3,2,1,0:T(8,128)(2,1)} all-to-all(bf16[16,1,128,2560]{3,2,1,0:T(8,128)(2,1)} %get-tuple-element.16), channel_id=1, replica_groups=mesh['grp_0'=2,'grp_1'=4,'grp_2'=2,'rep_0'=4,'rep_1'=2] {'grp_0','grp_1'..., dimensions={0} | all-to-all | bytes 20971520 | tf_op jit(solution)/shard_map/all_to_all | solution.py:30
  190.2 0.0 copy-start.2
  190.2 0.0 copy-start.1
  190.2 5.1 %all-to-all-start.4 = ((bf16[16,1,128,2560]{3,2,1,0:T(8,128)(2,1)}), bf16[16,1,128,2560]{3,2,1,0:T(8,128)(2,1)}, u32[]{:S(2)}, u32[]{:S(2)}) async-start(bf16[16,1,128,2560]{3,2,1,0:T(8,128)(2,1)} %get-tuple-element.15), calls=%async_computation.4 | async-start | bytes 20971520 | tf_op jit(solution)/shard_map/all_to_all | solution.py:30
  195.3 0.0 copy-done.2
  195.4 0.1 fusion.21
  195.5 0.0 copy-done.1
  195.5 0.5 fusion.6
  196.0 9.9 %select_reduce_fusion = (f32[384]{0:T(512)S(1)}, f32[384,2048]{1,0:T(8,128)}) fusion(pred[2048]{0:T(1024)(128)(4,1)S(1)} %fusion.21, bf16[2048,2560]{1,0:T(8,128)(2,1)} %fusion.1, bf16[384,2560]{1,0:T(8,128)(2,1)S(1)} %copy-done.1, f32[384]{0:T(512)S(1)} %add_rsqrt_fusion.1), kind=kOutput, calls=%fused_computation.19 | convolution fusion | flops 4031839744 | bytes 15602688 | tf_op jit(solution)/shard_map/dot_general | solution.py:63
  205.9 5.1 %gather_fusion.1 = f32[384]{0:T(512)S(1)} fusion(f32[384,2048]{1,0:T(8,128)} %get-tuple-element.24, s32[384]{0:T(512)S(1)} %fusion.28), kind=kCustom, calls=%fused_computation.1 | custom fusion | bytes 6144 | tf_op jit(solution)/shard_map/jit(take_along_axis)/gather | solution.py:74
  211.0 0.4 reduce.6
  211.4 0.4 reduce.7
  211.8 0.1 iota_compare_fusion.3
  211.9 0.1 iota_compare_fusion.2
  211.9 8.5 %fusion.9 = f32[384]{0:T(512)S(1)} fusion(pred[16,128]{1,0:T(8,128)(4,1)S(1)} %iota_compare_fusion.3, bf16[16,1,128,2560]{3,2,1,0:T(8,128)(2,1)} %all_to_all.37, bf16[384,2560]{1,0:T(8,128)(2,1)S(1)} %copy-done.1, f32[384]{0:T(512)S(1)} %add_rsqrt_fusion.1), kind=kOutput, calls=%fused_computation.18 | convolution fusion | flops 4031839744 | bytes 12456960 | tf_op jit(solution)/shard_map/qd,skrd->kqsr/dot_general | solution.py:101
  220.4 0.0 copy-start.3
  220.5 129.3 %all-to-all-done.4 = bf16[16,1,128,2560]{3,2,1,0:T(8,128)(2,1)} async-done(((bf16[16,1,128,2560]{3,2,1,0:T(8,128)(2,1)}), bf16[16,1,128,2560]{3,2,1,0:T(8,128)(2,1)}, u32[]{:S(2)}, u32[]{:S(2)}) %all-to-all-start.4) | async-done | bytes 10485792 | tf_op jit(solution)/shard_map/all_to_all | solution.py:30
  349.8 8.5 %fusion.8 = f32[384]{0:T(512)S(1)} fusion(pred[16,128]{1,0:T(8,128)(4,1)S(1)} %iota_compare_fusion.2, bf16[16,1,128,2560]{3,2,1,0:T(8,128)(2,1)} %all-to-all-done.4, bf16[384,2560]{1,0:T(8,128)(2,1)S(1)} %copy-done.1, f32[384]{0:T(512)S(1)} %add_rsqrt_fusion.1), kind=kOutput, calls=%fused_computation.16 | convolution fusion | flops 4031839744 | bytes 12456960 | tf_op jit(solution)/shard_map/qd,skrd->kqsr/dot_general | solution.py:101
  358.3 0.0 copy-done.3
  358.3 1.2 fusion.36
  359.5 5.6 %all-reduce.4 = (f32[]{:T(128)}, f32[]{:T(128)}) all-reduce(f32[]{:T(128)} %get-tuple-element.3, f32[]{:T(128)} %get-tuple-element.2), channel_id=1, replica_groups=mesh['grp_0'=2,'grp_1'=4,'grp_2'=2,'rep_0'=4,'rep_1'=2] {'grp_0'}, use_global_device_ids=true, to_apply=%region_9.10 | all-reduce | flops 2 | bytes 16 | tf_op jit(solution)/shard_map/psum | solution.py:40
  365.1 17.8 %all-reduce.1 = (f32[]{:T(128)}, f32[]{:T(128)}) all-reduce(f32[]{:T(128)} %get-tuple-element.12, f32[]{:T(128)} %get-tuple-element.13), channel_id=1, replica_groups=mesh['grp_0'=2,'grp_1'=4,'grp_2'=2,'rep_0'=4,'rep_1'=2] {'grp_1'}, use_global_device_ids=true, to_apply=%region_10.11 | all-reduce | flops 2 | bytes 16 | tf_op jit(solution)/shard_map/psum | solution.py:40
  382.9 3.2 all-reduce.3
  386.0 11.4 %all-reduce = (f32[]{:T(128)}, f32[]{:T(128)}) all-reduce(f32[]{:T(128)} %get-tuple-element.10, f32[]{:T(128)} %get-tuple-element.11), channel_id=1, replica_groups=mesh['grp_0'=2,'grp_1'=4,'grp_2'=2,'rep_0'=4,'rep_1'=2] {'rep_0'}, use_global_device_ids=true, to_apply=%region_12.13 | all-reduce | flops 2 | bytes 16 | tf_op jit(solution)/shard_map/psum | solution.py:40
  397.4 7.1 %all-reduce.2 = (f32[]{:T(128)}, f32[]{:T(128)}) all-reduce(f32[]{:T(128)} %get-tuple-element.4, f32[]{:T(128)} %get-tuple-element.5), channel_id=1, replica_groups=mesh['grp_0'=2,'grp_1'=4,'grp_2'=2,'rep_0'=4,'rep_1'=2] {'rep_1'}, use_global_device_ids=true, to_apply=%region_13.14 | all-reduce | flops 2 | bytes 16 | tf_op jit(solution)/shard_map/psum | solution.py:40
  (12 shorter events, 0.1 us)
Async XLA Ops:
  5.6 18.9 %all-to-all-start = ((s32[16,1,2]{2,1,0:T(1,128)}), s32[16,1,2]{2,1,0:T(1,128)S(1)}, u32[]{:S(2)}, u32[]{:S(2)}) async-start(s32[16,1,2]{2,1,0:T(1,128)} %copy.31), calls=%async_computation | async-start | bytes 16384 | tf_op jit(solution)/shard_map/all_to_all | solution.py:88
  12.0 7.0 %copy-start = (bf16[2048,2560]{1,0:T(8,128)(2,1)S(1)}, bf16[2048,2560]{1,0:T(8,128)(2,1)}, u32[]{:S(2)}) copy-start(bf16[2048,2560]{1,0:T(8,128)(2,1)} %param.7) | copy-start | bytes 31457284
  19.0 5.6 %copy-start.4 = (s32[16]{0:T(128)S(1)}, s32[16]{0:T(128)}, u32[]{:S(2)}) copy-start(s32[16]{0:T(128)} %param.8) | copy-start | bytes 196
  25.5 19.2 %all-to-all-start.1 = ((s32[16,1,1]{2,1,0:T(1,128)}), s32[16,1,1]{2,1,0:T(1,128)S(1)}, u32[]{:S(2)}, u32[]{:S(2)}) async-start(s32[16,1,1]{2,1,0:T(1,128)} %copy.34), calls=%async_computation.1 | async-start | bytes 16384 | tf_op jit(solution)/shard_map/all_to_all | solution.py:30
  44.7 22.1 %all-to-all-start.3 = ((s32[16,1,1]{2,1,0:T(1,128)}), s32[16,1,1]{2,1,0:T(1,128)S(1)}, u32[]{:S(2)}, u32[]{:S(2)}) async-start(s32[16,1,1]{2,1,0:T(1,128)} %copy.36), calls=%async_computation.3 | async-start | bytes 16384 | tf_op jit(solution)/shard_map/all_to_all | solution.py:30
  190.2 5.2 %copy-start.2 = (s32[384]{0:T(512)S(1)}, s32[384]{0:T(512)}, u32[]{:S(2)}) copy-start(s32[384]{0:T(512)} %param.9) | copy-start | bytes 4612
  190.2 5.3 %copy-start.1 = (bf16[384,2560]{1,0:T(8,128)(2,1)S(1)}, bf16[384,2560]{1,0:T(8,128)(2,1)}, u32[]{:S(2)}) copy-start(bf16[384,2560]{1,0:T(8,128)(2,1)} %param.6) | copy-start | bytes 5898244
  190.2 159.6 %all-to-all-start.4 = ((bf16[16,1,128,2560]{3,2,1,0:T(8,128)(2,1)}), bf16[16,1,128,2560]{3,2,1,0:T(8,128)(2,1)}, u32[]{:S(2)}, u32[]{:S(2)}) async-start(bf16[16,1,128,2560]{3,2,1,0:T(8,128)(2,1)} %get-tuple-element.15), calls=%async_computation.4 | async-start | bytes 20971520 | tf_op jit(solution)/shard_map/all_to_all | solution.py:30
  220.4 137.8 %copy-start.3 = (f32[384]{0:T(512)S(1)}, f32[384]{0:T(512)}, u32[]{:S(2)}) copy-start(f32[384]{0:T(512)} %param.11) | copy-start | bytes 4612
where the time goes:
time: 408 us; the launch traced here: 407 us
  blocking collectives  168 us (41%)
  waiting for transfers between devices  129 us (32%)
  local copies, waits for them, and re-layouts  39.1 us (10%)
  matrix products  26.9 us (7%)
  starting transfers between devices  23.1 us (6%)
  other arithmetic  16.8 us (4%)
    all_to_all x3, waiting for transfers between devices, grouped_exchange(): lax.all_to_all(group, axis, split_axis=split_dim, concat_axis=concat_dim,...  129 us
    all_to_all x1, blocking collectives, grouped_exchange(): lax.all_to_all(group, axis, split_axis=split_dim, concat_axis=concat_dim,...  123 us
    psum x5, blocking collectives, by_axis(): shard = lax.psum(shard, axis)  45 us
    dot_general x2, matrix products, score_blocks(): jnp.einsum('qd,skrd->kqsr', question_unit_vectors, arrived, preferred_ele...  17 us
    all_to_all x3, starting transfers between devices, grouped_exchange(): lax.all_to_all(group, axis, split_axis=split_dim, concat_axis=concat_dim,...  16.7 us
    slice x1, local copies, waits for them, and re-layouts, grouped_exchange(): lax.slice_in_dim(a, k * (items // count), (k + 1) * (items // count), axi...  16.3 us
    gather x1, local copies, waits for them, and re-layouts, local(): picked = unit_blocks[safe_block]  12.6 us
    dot_general x1, matrix products, local(): lax.dot_general(question_unit_vectors, document_unit_vectors, (((1,), (1,...  9.94 us
  transfers between devices with their start and end apart: 4, of which 1 were waited for; matrix products, arithmetic and copies ran while one was open for 16% of the time, Pallas kernels for 0%

commit v1 on v0

v1 whole, which is shorter than its diff:
```python
import jax
import jax.numpy as jnp
from jax import lax
from jax.experimental import pallas as pl
from jax.experimental.pallas import tpu as pltpu
from jax.sharding import Mesh
from jax.sharding import PartitionSpec as P


SIDE = "grp_0"
RING = "grp_1"
CORE = "grp_2"
PLANE = ("grp_0", "grp_1")
GRP_REP = ("grp_0", "grp_1", "grp_2", "rep_0", "rep_1")

inverse_softmax_sharpness = 20.0
norm_epsilon = 1e-06
LOCAL_BLOCKS = 2
SLOTS = 2

NT = (((1,), (1,)), ((), ()))
NEIGHBOURS = ((0, -1), (0, 1), (1, 0), (1, -1), (1, 1), (0, 2), (1, 2))


def normalize(rows):
    values = rows.astype(jnp.float32)
    scale = lax.rsqrt(jnp.sum(values * values, axis=-1, keepdims=True) + norm_epsilon)
    return (values * scale).astype(jnp.bfloat16)


def units_kernel(queries, first, second, pair, third):
    rows = first.shape[0]
    for k, piece in enumerate((first, second, third)):
        unit = normalize(queries[k * rows : (k + 1) * rows, :])
        piece[...] = unit
        if k < 2:
            pair[k * rows : (k + 1) * rows, :] = unit


def query_units(queries):
    rows, width = queries.shape
    third = rows // 3
    shape = lambda n: jax.ShapeDtypeStruct((n, width), jnp.bfloat16)
    return pl.pallas_call(
        units_kernel,
        out_shape=[shape(third), shape(third), shape(2 * third), shape(third)],
        cost_estimate=pl.CostEstimate(
            flops=3 * rows * width, transcendentals=rows, bytes_accessed=6 * rows * width
        ),
        name="query_units",
    )(queries)


def local_kernel(counts, pair, third, positive, passages, units, total, score, questions):
    step = pl.program_id(0)
    rows = passages.shape[0]
    block_rows = rows // LOCAL_BLOCKS

    @pl.when(step == 0)
    def _():
        questions[: pair.shape[0], :] = pair[...]
        questions[pair.shape[0] :, :] = third[...]
        total[...] = jnp.zeros_like(total)
        score[...] = jnp.zeros_like(score)

    units[...] = normalize(passages[...])
    similarity = (
        lax.dot_general(units[...], questions[...], NT, preferred_element_type=jnp.float32)
        * inverse_softmax_sharpness
    )
    row = lax.broadcasted_iota(jnp.int32, similarity.shape, 0)
    score[...] += jnp.sum(
        jnp.where(row + step * rows == positive[...], similarity, 0.0), axis=0, keepdims=True
    )
    kept = jnp.exp(similarity)
    for k in range(LOCAL_BLOCKS):
        part = slice(k * block_rows, (k + 1) * block_rows)
        inside = row[:block_rows] < counts[step * LOCAL_BLOCKS + k]
        total[...] += jnp.sum(jnp.where(inside, kept[part], 0.0), axis=0, keepdims=True)


def score_local(counts, pair, third, positive, passages):
    local_rows, width = passages.shape
    blocks = counts.shape[0]
    step_rows = local_rows // blocks * LOCAL_BLOCKS
    steps = blocks // LOCAL_BLOCKS
    rows = positive.shape[1]
    piece = lambda a: pl.BlockSpec(a.shape, lambda s, c: (0, 0))
    line = pl.BlockSpec((1, rows), lambda s, c: (0, 0))
    band = pl.BlockSpec((step_rows, width), lambda s, c: (s, 0))
    return pl.pallas_call(
        local_kernel,
        grid_spec=pltpu.PrefetchScalarGridSpec(
            num_scalar_prefetch=1,
            grid=(steps,),
            in_specs=[piece(pair), piece(third), line, band],
            out_specs=[band, line, line],
            scratch_shapes=[pltpu.VMEM((rows, width), jnp.bfloat16)],
        ),
        out_shape=[
            jax.ShapeDtypeStruct(passages.shape, jnp.bfloat16),
            jax.ShapeDtypeStruct((1, rows), jnp.float32),
            jax.ShapeDtypeStruct((1, rows), jnp.float32),
        ],
        cost_estimate=pl.CostEstimate(
            flops=2 * local_rows * width * rows,
            transcendentals=local_rows * rows,
            bytes_accessed=4 * local_rows * width,
        ),
        name="score_local",
    )(counts, pair, third, positive, passages)


def listed_kernel(jobs, early, table, *refs):
    pieces = refs[: sum(len(job) for job in jobs)]
    done = refs[len(pieces) : len(pieces) + len(early)]
    mine, twin = refs[len(pieces) + len(early) :][:2]
    totals = refs[len(pieces) + len(early) + 2 : -2]
    keys, sems = refs[-2:]
    block_rows = mine.shape[1]

    def copies(j, source):
        found = []
        for s in range(2 * SLOTS):
            home = mine if s < SLOTS else twin
            found.append(
                pltpu.make_async_copy(
                    home.at[table[source * 4 * SLOTS + s]],
                    keys.at[j, pl.ds(s * block_rows, block_rows)],
                    sems.at[j, s],
                )
            )
        return found

    sources = [job[0][0] for job in jobs]
    started = [copies(j, source) for j, source in enumerate(sources)]
    for group in started:
        for copy in group:
            copy.start()
    for k, (j, first) in enumerate(early):
        totals[j][:, first : first + done[k].shape[1]] = done[k][...]
    at = 0
    for j, job in enumerate(jobs):
        for copy in started[j]:
            copy.wait()
        for source, first in job:
            piece = pieces[at]
            at += 1
            similarity = (
                lax.dot_general(keys[j], piece[...], NT, preferred_element_type=jnp.float32)
                * inverse_softmax_sharpness
            )
            kept = jnp.exp(similarity)
            row = lax.broadcasted_iota(jnp.int32, (block_rows, piece.shape[0]), 0)
            added = jnp.zeros((1, piece.shape[0]), jnp.float32)
            for s in range(2 * SLOTS):
                inside = row < table[source * 4 * SLOTS + 2 * SLOTS + s]
                part = kept[s * block_rows : (s + 1) * block_rows]
                added += jnp.sum(jnp.where(inside, part, 0.0), axis=0, keepdims=True)
            totals[j][:, first : first + piece.shape[0]] = added


def score_listed(table, mine, twin, jobs, early=()):
    plan, pieces, sizes = [], [], []
    taken = {}
    for k, first, line in early:
        taken[k] = max(taken.get(k, 0), first + line.shape[1])
    for j, (source, job) in enumerate(jobs):
        first = taken.get(j, 0)
        rows = []
        for piece in job:
            rows.append((source, first))
            pieces.append(piece)
            first += piece.shape[0]
        plan.append(tuple(rows))
        sizes.append(first)
    width = mine.shape[2]
    block_rows = mine.shape[1]
    amount = sum(piece.shape[0] for piece in pieces)
    vmem = pl.BlockSpec(memory_space=pltpu.VMEM)
    hbm = pl.BlockSpec(memory_space=pltpu.HBM)
    kernel = lambda *refs: listed_kernel(plan, [(j, first) for j, first, _ in early], *refs)
    return pl.pallas_call(
        kernel,
        in_specs=[pl.BlockSpec(memory_space=pltpu.SMEM)]
        + [vmem] * (len(pieces) + len(early))
        + [hbm, hbm],
        out_specs=[vmem] * len(jobs),
        out_shape=[jax.ShapeDtypeStruct((1, n), jnp.float32) for n in sizes],
        scratch_shapes=[
            pltpu.VMEM((len(jobs), 2 * SLOTS * block_rows, width), jnp.bfloat16),
            pltpu.SemaphoreType.DMA((len(jobs), 2 * SLOTS)),
        ],
        cost_estimate=pl.CostEstimate(
            flops=4 * SLOTS * block_rows * width * amount,
            transcendentals=2 * SLOTS * block_rows * amount,
            bytes_accessed=len(jobs) * 4 * SLOTS * block_rows * width + 2 * amount * width,
        ),
        name="score_listed",
    )(table, *pieces, *[line for _, _, line in early], mine, twin)


def slot_table(lists, device, blocks_here, counts):
    owner = lists // blocks_here
    block = lists % blocks_here
    mine = owner == device
    first = jnp.max(jnp.where(mine, block, -1), axis=1)
    second = jnp.min(jnp.where(mine, block, blocks_here), axis=1)
    second = jnp.where(jnp.sum(mine, axis=1) > 1, second, -1)
    index = jnp.stack([first, second], axis=1)
    choice = index[:, :, None] == jnp.arange(blocks_here, dtype=jnp.int32)[None, None, :]
    kept = jnp.sum(jnp.where(choice, counts[None, None, :], 0), axis=2)
    return jnp.maximum(index, 0), kept


def local(queries, passages, block_valid_counts, positive_index, neg_blocks, query_weights):
    _, width = queries.shape
    blocks_here = block_valid_counts.shape[0]
    ring = lax.axis_size(RING)
    replicas = lax.axis_size("rep_0") * lax.axis_size("rep_1")
    device = lax.axis_index(GRP_REP)

    def forward(a):
        return lax.ppermute(a, RING, [(i, (i + 1) % ring) for i in range(ring)])

    def backward(a):
        return lax.ppermute(a, RING, [(i, (i - 1) % ring) for i in range(ring)])

    def across(a):
        return lax.ppermute(a, SIDE, [(0, 1), (1, 0)])

    def swap(a):
        return lax.ppermute(a, CORE, [(0, 1), (1, 0)])

    def home(a, dx, dz):
        pairs = []
        for i in range(2 * ring):
            x, z = divmod(i, ring)
            pairs.append((i, (x ^ dx) * ring + (z + dz) % ring))
        return lax.ppermute(a, PLANE, pairs)

    a, b, ab, c = query_units(queries)
    below_a = forward(a)
    above_ab = backward(ab)
    beside_c = across(c)
    lists = [neg_blocks]
    for dx, dz in NEIGHBOURS:
        lists.append(home(neg_blocks, dx, -dz))
    twin_counts = swap(block_valid_counts)
    below_b = forward(b)
    below_c = forward(c)
    above_c = backward(c)
    beside_ab = across(ab)

    beside_below_a = across(below_a)
    beside_below_b = across(below_b)
    beside_above_ab = across(above_ab)
    beside_below_c = forward(beside_c)
    beside_above_c = backward(beside_c)
    facing_c = forward(below_c)
    facing_ab = backward(above_ab)
    beside_facing_a = forward(beside_below_a)
    beside_facing_b = forward(beside_below_b)
    beside_facing_c = backward(beside_above_c)

    positive = positive_index[None, :]
    units, local_total, positive_score = score_local(block_valid_counts, ab, c, positive, passages)
    blocks = units.reshape(blocks_here, -1, width)
    twin = swap(blocks)

    listed = jnp.concatenate(lists, axis=0)
    index_mine, kept_mine = slot_table(listed, device, blocks_here, block_valid_counts)
    index_twin, kept_twin = slot_table(listed, device ^ replicas, blocks_here, twin_counts)
    table = jnp.concatenate([index_mine, index_twin, kept_mine, kept_twin], axis=1).reshape(-1)

    def score(jobs, early=()):
        return score_listed(table, blocks, twin, jobs, early)

    (own_total,) = score([(0, [ab, c])])
    (total_1,) = score([(1, [below_a, below_b, below_c])])
    (total_2,) = score([(2, [above_ab, above_c])])
    (total_3,) = score([(3, [beside_ab, beside_c])])
    (total_4,) = score([(4, [beside_below_a, beside_below_b, beside_below_c])])
    (total_6,) = score([(6, [facing_ab, facing_c])])
    (early_7,) = score([(7, [beside_facing_a])])
    total_5, total_7 = score(
        [(5, [beside_above_ab, beside_above_c]), (7, [beside_facing_b, beside_facing_c])],
        [(1, 0, early_7)],
    )
    totals = [total_1, total_2, total_3, total_4, total_5, total_6, total_7]
    total = local_total + own_total
    for k, (dx, dz) in enumerate(NEIGHBOURS):
        total += home(totals[k], dx, dz)
    query_loss = (jnp.log(total) - positive_score)[0]
    sums = jnp.stack([jnp.sum(query_weights * query_loss), jnp.sum(query_weights)])
    everyone = lax.axis_size(GRP_REP)
    shares = lax.all_to_all(
        jnp.broadcast_to(sums[None, :], (everyone, 2)),
        GRP_REP,
        split_axis=0,
        concat_axis=0,
        tiled=True,
    )
    sums = jnp.sum(shares, axis=0)
    return (query_loss, sums[0] / sums[1])


def solution(mesh):
    split = Mesh(mesh.devices.reshape(2, 4, 2, 4, 2), GRP_REP)
    in_specs = (
        P(GRP_REP, None),
        P(GRP_REP, None),
        P(GRP_REP),
        P(GRP_REP),
        P(GRP_REP, None),
        P(GRP_REP),
    )
    out_specs = (P(GRP_REP), P())

    return jax.shard_map(local, mesh=split, in_specs=in_specs, out_specs=out_specs, check_vma=False)
```

time: 408 us -> 231 us (0.57)
  blocking collectives: 168 us -> 18.8 us
  Pallas kernels: 0 us -> 62.6 us
  local copies, waits for them, and re-layouts: 39.1 us -> 3.04 us
  waiting for transfers between devices: 129 us -> 97 us
  matrix products: 26.9 us -> 0 us
  starting transfers between devices: 23.1 us -> 41.6 us
  other arithmetic: 16.8 us -> 3.4 us
    all_to_all x4 -> x0, waiting for transfers between devices: 129 us -> none  [the longest x3 129 us: grouped_exchange(): lax.all_to_all(group, axis, split_axis=split_dim, concat_axis=concat_dim,...]
    all_to_all x1, blocking collectives: 123 us -> 18.8 us  [local(): lax.all_to_all(jnp.broadcast_to(sums[None, :], (everyone, 2)), GRP_REP, s...]
    ppermute x0 -> x33, waiting for transfers between devices: none -> 97 us  [the longest x7 50 us: forward(): return lax.ppermute(a, RING, [(i, (i + 1) % ring) for i in range(ring)])]
    pallas_call x0 -> x10, Pallas kernels: none -> 62.6 us  [the longest x8 44.9 us: score_listed(): pl.pallas_call(kernel, in_specs=[pl.BlockSpec(memory_space=pltpu.SMEM)] +...]
    psum x5 -> x0, blocking collectives: 45 us -> none  [by_axis(): shard = lax.psum(shard, axis)]
    ppermute x0 -> x33, starting transfers between devices: none -> 41.6 us  [the longest x14 23.8 us: home(): return lax.ppermute(a, PLANE, pairs)]
    dot_general x3 -> x0, matrix products: 26.9 us -> none  [the longest x2 17 us: score_blocks(): jnp.einsum('qd,skrd->kqsr', question_unit_vectors, arrived, preferred_ele...]
    all_to_all x4 -> x0, starting transfers between devices: 23.1 us -> none  [the longest x3 16.7 us: grouped_exchange(): lax.all_to_all(group, axis, split_axis=split_dim, concat_axis=concat_dim,...]
  transfers between devices with their start and end apart: 4 -> 33, of which waited for: 1 -> 12; matrix products, arithmetic and copies ran while one was open for 16% -> 1% of each run, Pallas kernels for 0% -> 20%
where the time goes in v1:
time: 231 us; the launch traced here: 230 us
  waiting for transfers between devices  97 us (42%)
  Pallas kernels  62.6 us (27%)
  starting transfers between devices  41.6 us (18%)
  blocking collectives  18.8 us (8%)
  other arithmetic  3.4 us (1%)
  between operations  3.4 us (1%)
  local copies, waits for them, and re-layouts  3.04 us (1%)
    ppermute x7, waiting for transfers between devices, forward(): return lax.ppermute(a, RING, [(i, (i + 1) % ring) for i in range(ring)])  50 us
    pallas_call x8, Pallas kernels, score_listed(): pl.pallas_call(kernel, in_specs=[pl.BlockSpec(memory_space=pltpu.SMEM)] +...  44.9 us
    ppermute x5, waiting for transfers between devices, across(): return lax.ppermute(a, SIDE, [(0, 1), (1, 0)])  31.9 us
    ppermute x14, starting transfers between devices, home(): return lax.ppermute(a, PLANE, pairs)  23.8 us
    all_to_all x1, blocking collectives, local(): lax.all_to_all(jnp.broadcast_to(sums[None, :], (everyone, 2)), GRP_REP, s...  18.8 us
    pallas_call x1, Pallas kernels, score_local(): pl.pallas_call(local_kernel, grid_spec=pltpu.PrefetchScalarGridSpec(num_s...  13.9 us
    ppermute x2, waiting for transfers between devices, swap(): return lax.ppermute(a, CORE, [(0, 1), (1, 0)])  11 us
    ppermute x5, starting transfers between devices, backward(): return lax.ppermute(a, RING, [(i, (i - 1) % ring) for i in range(ring)])  6.6 us
  transfers between devices with their start and end apart: 33, of which 12 were waited for; matrix products, arithmetic and copies ran while one was open for 1% of the time, Pallas kernels for 20%

profile of v1, /device:TPU:0, one launch (start us, length us, event | category | flops | bytes accessed | tf_op | source)
XLA Modules:
  0.0 229.8 jit_solution(12850249484388337084)
XLA Ops:
  0.6 3.8 %query_units.1 = (bf16[128,2560]{1,0:T(8,128)(2,1)}, bf16[128,2560]{1,0:T(8,128)(2,1)}, bf16[256,2560]{1,0:T(8,128)(2,1)}, bf16[128,2560]{1,0:T(8,128)(2,1)}) custom-call(bf16[384,2560]{1,0:T(8,128)(2,1)} %queries.1), custom_call_target="tpu_custom_call" | custom-call | flops 2949120 | bytes 5898240 | tf_op jit(solution)/shard_map/query_units/pallas_call | solution.py:44
  4.4 0.6 broadcast_in_dim.43.positive
  5.0 13.9 %score_local.1 = (bf16[2048,2560]{1,0:T(8,128)(2,1)}, f32[1,384]{1,0:T(1,128)}, f32[1,384]{1,0:T(1,128)}) custom-call(s32[16]{0:T(128)} %counts.1, bf16[256,2560]{1,0:T(8,128)(2,1)} %get-tuple-element.11.pair.refs_1_, bf16[128,2560]{1,0:T(8,128)(2,1)} %get-tuple-element.12.third.refs_2_, s32[1,384]{1,0:T(1,128)} %broadcast_in_dim.43.positive, ...), custom_call_target="tpu_custom_call" | custom-call | flops 4026531840 | bytes 20971520 | tf_op jit(solution)/shard_map/score_local/pallas_call | solution.py:91
  18.9 2.1 collective-permute-start.11
  21.0 0.1 collective-permute-start.7
  21.2 1.9 collective-permute-start
  23.1 1.3 collective-permute-start.1
  24.4 11.0 %collective-permute-done.7 = s32[16]{0:T(128)S(1)} collective-permute-done((s32[16]{0:T(128)S(1)}, s32[16]{0:T(128)S(1)}, u32[]{:S(2)}, u32[]{:S(2)}) %collective-permute-start.7) | collective-permute-done | bytes 96 | tf_op jit(solution)/shard_map/ppermute | solution.py:233
  35.4 1.6 collective-permute-start.2
  37.0 1.5 collective-permute-done
  38.5 0.6 collective-permute-start.3
  39.1 3.6 %collective-permute-start.4 = (s32[1,28]{1,0:T(1,128)S(1)}, s32[1,28]{1,0:T(1,128)S(1)}, u32[]{:S(2)}, u32[]{:S(2)}) collective-permute-start(s32[1,28]{1,0:T(1,128)S(1)} %copy-done.17), channel_id=1, source_target_pairs={{0,112},{16,64},{32,80},{48,96},{64,48},{80,0},{96,16},{112,32},{1... | collective-permute-start | bytes 344 | tf_op jit(solution)/shard_map/ppermute | solution.py:240
  42.7 1.1 collective-permute-start.5
  43.8 0.4 collective-permute-done.3
  44.2 2.9 %collective-permute-start.6 = (s32[1,28]{1,0:T(1,128)S(1)}, s32[1,28]{1,0:T(1,128)S(1)}, u32[]{:S(2)}, u32[]{:S(2)}) collective-permute-start(s32[1,28]{1,0:T(1,128)S(1)} %copy-done.17), channel_id=1, source_target_pairs={{0,96},{16,112},{32,64},{48,80},{64,32},{80,48},{96,0},{112,16},{1... | collective-permute-start | bytes 344 | tf_op jit(solution)/shard_map/ppermute | solution.py:240
  47.1 0.6 collective-permute-done.5
  47.7 0.9 collective-permute-start.9
  48.6 1.5 collective-permute-done.6
  50.2 1.3 collective-permute-start.13
  51.5 1.0 collective-permute-start.16
  52.5 13.8 %collective-permute-done.10.refs_2_ = bf16[128,2560]{1,0:T(8,128)(2,1)} collective-permute-done((bf16[128,2560]{1,0:T(8,128)(2,1)}, bf16[128,2560]{1,0:T(8,128)(2,1)}, u32[]{:S(2)}, u32[]{:S(2)}) %collective-permute-start.10) | collective-permute-done | bytes 655392 | tf_op jit(solution)/shard_map/ppermute | solution.py:224
  66.3 0.5 collective-permute-start.17
  66.8 11.2 %collective-permute-done.9.refs_1_ = bf16[128,2560]{1,0:T(8,128)(2,1)} collective-permute-done((bf16[128,2560]{1,0:T(8,128)(2,1)}, bf16[128,2560]{1,0:T(8,128)(2,1)}, u32[]{:S(2)}, u32[]{:S(2)}) %collective-permute-start.9) | collective-permute-done | bytes 655392 | tf_op jit(solution)/shard_map/ppermute | solution.py:224
  78.0 16.0 %collective-permute-done.17.refs_2_ = bf16[128,2560]{1,0:T(8,128)(2,1)} collective-permute-done((bf16[128,2560]{1,0:T(8,128)(2,1)S(1)}, bf16[128,2560]{1,0:T(8,128)(2,1)}, u32[]{:S(2)}, u32[]{:S(2)}) %collective-permute-start.17) | collective-permute-done | bytes 655392 | tf_op jit(solution)/shard_map/ppermute | solution.py:230
  94.0 0.3 collective-permute-start.21
  94.2 1.5 collective-permute-start.19
  95.7 0.6 collective-permute-start.20
  96.4 3.0 %collective-permute-start.24 = (bf16[128,2560]{1,0:T(8,128)(2,1)}, bf16[128,2560]{1,0:T(8,128)(2,1)}, u32[]{:S(2)}, u32[]{:S(2)}) collective-permute-start(bf16[128,2560]{1,0:T(8,128)(2,1)} %collective-permute-done.17.refs_2_), channel_id=1, source_target_pairs={{0,48},{16,0},{32,16},{48,32},{1,49},{17,1},{33,17},{49,33},{2,50}... | collective-permute-start | bytes 1966088 | tf_op jit(solution)/shard_map/ppermute | solution.py:227
  99.4 8.7 %collective-permute-done.21.refs_3_ = bf16[128,2560]{1,0:T(8,128)(2,1)} collective-permute-done((bf16[128,2560]{1,0:T(8,128)(2,1)}, bf16[128,2560]{1,0:T(8,128)(2,1)}, u32[]{:S(2)}, u32[]{:S(2)}) %collective-permute-start.21) | collective-permute-done | bytes 655392 | tf_op jit(solution)/shard_map/ppermute | solution.py:224
  108.2 0.5 collective-permute-start.29
  108.7 3.5 %collective-permute-done.19.refs_1_ = bf16[128,2560]{1,0:T(8,128)(2,1)} collective-permute-done((bf16[128,2560]{1,0:T(8,128)(2,1)}, bf16[128,2560]{1,0:T(8,128)(2,1)}, u32[]{:S(2)}, u32[]{:S(2)}) %collective-permute-start.19) | collective-permute-done | bytes 655392 | tf_op jit(solution)/shard_map/ppermute | solution.py:230
  112.2 1.5 collective-permute-start.23
  113.7 12.4 %collective-permute-done.20.refs_2_ = bf16[128,2560]{1,0:T(8,128)(2,1)S(1)} collective-permute-done((bf16[128,2560]{1,0:T(8,128)(2,1)}, bf16[128,2560]{1,0:T(8,128)(2,1)S(1)}, u32[]{:S(2)}, u32[]{:S(2)}) %collective-permute-start.20) | collective-permute-done | bytes 655392 | tf_op jit(solution)/shard_map/ppermute | solution.py:230
  126.1 1.0 collective-permute-start.27
  127.1 0.2 select_reduce_fusion.5
  127.3 0.2 select_reduce_fusion.1
  127.5 1.3 collective-permute-start.30
  128.9 16.2 %collective-permute-done.27.refs_1_ = bf16[128,2560]{1,0:T(8,128)(2,1)S(1)} collective-permute-done((bf16[128,2560]{1,0:T(8,128)(2,1)}, bf16[128,2560]{1,0:T(8,128)(2,1)S(1)}, u32[]{:S(2)}, u32[]{:S(2)}) %collective-permute-start.27) | collective-permute-done | bytes 655392 | tf_op jit(solution)/shard_map/ppermute | solution.py:224
  145.1 1.8 collective-permute-start.26
  146.9 0.3 collective-permute-start.25
  147.2 0.2 select_reduce_fusion
  147.4 0.1 copy.12
  147.5 0.6 reshape.57.refs_0_
  148.1 4.2 %score_listed.13.refs_5_ = f32[1,128]{1,0:T(1,128)} custom-call(s32[64]{0:T(128)} %reshape.57.refs_0_, bf16[128,2560]{1,0:T(8,128)(2,1)} %copy-done.7, bf16[16,128,2560]{2,1,0:T(8,128)(2,1)} %bitcast.11, bf16[16,128,2560]{2,1,0:T(8,128)(2,1)} %collective-permute-done.8.refs_4_.refs_5_.refs_3_.refs_7_), custom_call_target="tpu_custom_call" | custom-call | flops 335544320 | bytes 3276800 | tf_op jit(solution)/shard_map/score_listed/pallas_call | solution.py:183
  152.3 6.0 %score_listed.9 = f32[1,384]{1,0:T(1,128)} custom-call(s32[64]{0:T(128)} %reshape.57.refs_0_, bf16[128,2560]{1,0:T(8,128)(2,1)} %collective-permute-done.9.refs_1_, bf16[128,2560]{1,0:T(8,128)(2,1)} %collective-permute-done.10.refs_2_, bf16[128,2560]{1,0:T(8,128)(2,1)} %copy-done.4, bf16[16,128,2560]{2,1,0:T(8,128)(2,1)} %bitcast.12, ...), custom_call_target="tpu_custom_call" | custom-call | flops 1006632960 | bytes 4587520 | tf_op jit(solution)/shard_map/score_listed/pallas_call | solution.py:183
  158.3 5.3 %score_listed.10 = f32[1,384]{1,0:T(1,128)} custom-call(s32[64]{0:T(128)} %reshape.57.refs_0_, bf16[256,2560]{1,0:T(8,128)(2,1)} %copy-done.1, bf16[128,2560]{1,0:T(8,128)(2,1)} %copy-done.6, bf16[16,128,2560]{2,1,0:T(8,128)(2,1)} %bitcast.13, bf16[16,128,2560]{2,1,0:T(8,128)(2,1)} %collective-permute-done.8.refs_4_.refs_5_.refs_3_.refs_7_), custom_call_target="tpu_custom_call" | custom-call | flops 1006632960 | bytes 4587520 | tf_op jit(solution)/shard_map/score_listed/pallas_call | solution.py:183
  163.7 5.3 %score_listed.11 = f32[1,384]{1,0:T(1,128)} custom-call(s32[64]{0:T(128)} %reshape.57.refs_0_, bf16[256,2560]{1,0:T(8,128)(2,1)} %collective-permute-done.16.refs_1_, bf16[128,2560]{1,0:T(8,128)(2,1)} %collective-permute-done.17.refs_2_, bf16[16,128,2560]{2,1,0:T(8,128)(2,1)} %bitcast.14, ...), custom_call_target="tpu_custom_call" | custom-call | flops 1006632960 | bytes 4587520 | tf_op jit(solution)/shard_map/score_listed/pallas_call | solution.py:183
  169.0 6.0 %score_listed.12 = f32[1,384]{1,0:T(1,128)} custom-call(s32[64]{0:T(128)} %reshape.57.refs_0_, bf16[128,2560]{1,0:T(8,128)(2,1)} %collective-permute-done.19.refs_1_, bf16[128,2560]{1,0:T(8,128)(2,1)} %copy-done.5, bf16[128,2560]{1,0:T(8,128)(2,1)} %collective-permute-done.21.refs_3_, bf16[16,128,2560]{2,1,0:T(8,128)(2,1)} %bitcast.15, ...), custom_call_target="tpu_custom_call" | custom-call | flops 1006632960 | bytes 4587520 | tf_op jit(solution)/shard_map/score_listed/pallas_call | solution.py:183
  175.0 0.0 copy-start.11
  175.0 3.1 %collective-permute-start.12 = (f32[1,384]{1,0:T(1,128)S(1)}, f32[1,384]{1,0:T(1,128)S(1)}, u32[]{:S(2)}, u32[]{:S(2)}) collective-permute-start(f32[1,384]{1,0:T(1,128)S(1)} %copy-done.14), channel_id=1, source_target_pairs={{0,48},{16,0},{32,16},{48,32},{64,112},{80,64},{96,80},{112,96},{1... | collective-permute-start | bytes 4616 | tf_op jit(solution)/shard_map/ppermute | solution.py:240
  178.1 5.3 %score_listed.15 = f32[1,384]{1,0:T(1,128)} custom-call(s32[64]{0:T(128)} %reshape.57.refs_0_, bf16[256,2560]{1,0:T(8,128)(2,1)} %collective-permute-done.29.refs_1_, bf16[128,2560]{1,0:T(8,128)(2,1)} %collective-permute-done.30.refs_2_, bf16[16,128,2560]{2,1,0:T(8,128)(2,1)} %bitcast.16, ...), custom_call_target="tpu_custom_call" | custom-call | flops 1006632960 | bytes 4587520 | tf_op jit(solution)/shard_map/score_listed/pallas_call | solution.py:183
  183.5 1.0 collective-permute-start.18
  184.5 3.8 %collective-permute-start.22 = (f32[1,384]{1,0:T(1,128)S(1)}, f32[1,384]{1,0:T(1,128)S(1)}, u32[]{:S(2)}, u32[]{:S(2)}) collective-permute-start(f32[1,384]{1,0:T(1,128)S(1)} %copy-done.11), channel_id=1, source_target_pairs={{0,112},{16,64},{32,80},{48,96},{64,48},{80,0},{96,16},{112,32},{1... | collective-permute-start | bytes 4616 | tf_op jit(solution)/shard_map/ppermute | solution.py:240
  188.3 1.1 copy-done.2
  189.3 7.3 %score_listed.14 = (f32[1,384]{1,0:T(1,128)}, f32[1,384]{1,0:T(1,128)}) custom-call(s32[64]{0:T(128)} %reshape.57.refs_0_, bf16[256,2560]{1,0:T(8,128)(2,1)} %copy-done.2, bf16[128,2560]{1,0:T(8,128)(2,1)} %collective-permute-done.24.refs_2_, bf16[128,2560]{1,0:T(8,128)(2,1)} %collective-permute-done.25.refs_3_, ...), custom_call_target="tpu_custom_call" | custom-call | flops 1677721600 | bytes 8519680 | tf_op jit(solution)/shard_map/score_listed/pallas_call | solution.py:183
  196.7 0.1 collective-permute-start.28
  196.8 2.9 %collective-permute-start.32 = (f32[1,384]{1,0:T(1,128)}, f32[1,384]{1,0:T(1,128)S(1)}, u32[]{:S(2)}, u32[]{:S(2)}) collective-permute-start(f32[1,384]{1,0:T(1,128)} %get-tuple-element.18), channel_id=1, source_target_pairs={{0,96},{16,112},{32,64},{48,80},{64,32},{80,48},{96,0},{112,16},{1... | collective-permute-start | bytes 4616 | tf_op jit(solution)/shard_map/ppermute | solution.py:240
  199.7 5.4 %score_listed.8 = f32[1,384]{1,0:T(1,128)} custom-call(s32[64]{0:T(128)} %reshape.57.refs_0_, bf16[256,2560]{1,0:T(8,128)(2,1)} %get-tuple-element.11.pair.refs_1_, bf16[128,2560]{1,0:T(8,128)(2,1)} %get-tuple-element.12.third.refs_2_, bf16[16,128,2560]{2,1,0:T(8,128)(2,1)} %bitcast.18, ...), custom_call_target="tpu_custom_call" | custom-call | flops 1006632960 | bytes 4587520 | tf_op jit(solution)/shard_map/score_listed/pallas_call | solution.py:183
  205.2 0.7 subtract_reduce_fusion
  205.9 0.6 multiply_reduce_fusion
  206.5 1.3 pad_maximum_fusion
  207.8 18.8 %all_to_all.6 = f32[128,1,2]{2,1,0:T(1,128)S(1)} all-to-all(f32[128,1,2]{2,1,0:T(1,128)S(1)} %broadcast_in_dim.48), channel_id=1, replica_groups=mesh['grp_0'=2,'grp_1'=4,'grp_2'=2,'rep_0'=4,'rep_1'=2] {'grp_0','grp_1'..., dimensions={0} | all-to-all | bytes 2048 | tf_op jit(solution)/shard_map/all_to_all | solution.py:297
  226.6 0.2 reduce_sum.69
  226.8 0.6 fusion.4
  (69 shorter events, 0.3 us)
Async XLA Ops:
  0.6 3.8 %copy-start.9 = (s32[384]{0:T(512)S(1)}, s32[384]{0:T(512)}, u32[]{:S(2)}) copy-start(s32[384]{0:T(512)} %param.9) | copy-start | bytes 4612
  5.0 13.9 %copy-start.3 = (bf16[128,2560]{1,0:T(8,128)(2,1)S(1)}, bf16[128,2560]{1,0:T(8,128)(2,1)}, u32[]{:S(2)}) copy-start(bf16[128,2560]{1,0:T(8,128)(2,1)} %get-tuple-element.12.third.refs_2_) | copy-start | bytes 1966084
  5.0 16.0 %copy-start.18 = (s32[16]{0:T(128)S(1)}, s32[16]{0:T(128)}, u32[]{:S(2)}) copy-start(s32[16]{0:T(128)} %counts.1) | copy-start | bytes 196
  5.0 16.2 %copy-start.17 = (s32[1,28]{1,0:T(1,128)S(1)}, s32[1,28]{1,0:T(1,128)}, u32[]{:S(2)}) copy-start(s32[1,28]{1,0:T(1,128)} %param.10) | copy-start | bytes 340
  5.0 45.2 %copy-start = (bf16[256,2560]{1,0:T(8,128)(2,1)S(1)}, bf16[256,2560]{1,0:T(8,128)(2,1)}, u32[]{:S(2)}) copy-start(bf16[256,2560]{1,0:T(8,128)(2,1)} %get-tuple-element.11.pair.refs_1_) | copy-start | bytes 3932164
  18.9 128.0 %collective-permute-start.8 = (bf16[16,128,2560]{2,1,0:T(8,128)(2,1)}, bf16[16,128,2560]{2,1,0:T(8,128)(2,1)}, u32[]{:S(2)}, u32[]{:S(2)}) collective-permute-start(bf16[16,128,2560]{2,1,0:T(8,128)(2,1)} %bitcast.10), channel_id=1, source_target_pairs={{0,8},{8,0},{1,9},{9,1},{2,10},{10,2},{3,11},{11,3},{4,12},{12,4},... | collective-permute-start | bytes 31457288 | tf_op jit(solution)/shard_map/ppermute | solution.py:233
  18.9 32.6 %collective-permute-start.11 = (bf16[128,2560]{1,0:T(8,128)(2,1)S(1)}, bf16[128,2560]{1,0:T(8,128)(2,1)S(1)}, u32[]{:S(2)}, u32[]{:S(2)}) collective-permute-start(bf16[128,2560]{1,0:T(8,128)(2,1)S(1)} %copy-done.3), channel_id=1, source_target_pairs={{0,16},{16,32},{32,48},{48,0},{1,17},{17,33},{33,49},{49,1},{2,18}... | collective-permute-start | bytes 1966088 | tf_op jit(solution)/shard_map/ppermute | solution.py:224
  21.0 14.4 %collective-permute-start.7 = (s32[16]{0:T(128)S(1)}, s32[16]{0:T(128)S(1)}, u32[]{:S(2)}, u32[]{:S(2)}) collective-permute-start(s32[16]{0:T(128)S(1)} %copy-done.18), channel_id=1, source_target_pairs={{0,8},{8,0},{1,9},{9,1},{2,10},{10,2},{3,11},{11,3},{4,12},{12,4},... | collective-permute-start | bytes 200 | tf_op jit(solution)/shard_map/ppermute | solution.py:233
  21.2 17.4 %collective-permute-start = (s32[1,28]{1,0:T(1,128)S(1)}, s32[1,28]{1,0:T(1,128)S(1)}, u32[]{:S(2)}, u32[]{:S(2)}) collective-permute-start(s32[1,28]{1,0:T(1,128)S(1)} %copy-done.17), channel_id=1, source_target_pairs={{0,16},{16,32},{32,48},{48,0},{64,80},{80,96},{96,112},{112,64},{1... | collective-permute-start | bytes 344 | tf_op jit(solution)/shard_map/ppermute | solution.py:240
  23.1 16.0 %collective-permute-start.1 = (s32[1,28]{1,0:T(1,128)S(1)}, s32[1,28]{1,0:T(1,128)S(1)}, u32[]{:S(2)}, u32[]{:S(2)}) collective-permute-start(s32[1,28]{1,0:T(1,128)S(1)} %copy-done.17), channel_id=1, source_target_pairs={{0,48},{16,0},{32,16},{48,32},{64,112},{80,64},{96,80},{112,96},{1... | collective-permute-start | bytes 344 | tf_op jit(solution)/shard_map/ppermute | solution.py:240
  35.4 7.3 %collective-permute-start.2 = (s32[1,28]{1,0:T(1,128)S(1)}, s32[1,28]{1,0:T(1,128)S(1)}, u32[]{:S(2)}, u32[]{:S(2)}) collective-permute-start(s32[1,28]{1,0:T(1,128)S(1)} %copy-done.17), channel_id=1, source_target_pairs={{0,64},{16,80},{32,96},{48,112},{64,0},{80,16},{96,32},{112,48},{1... | collective-permute-start | bytes 344 | tf_op jit(solution)/shard_map/ppermute | solution.py:240
  38.5 5.7 %collective-permute-start.3 = (s32[1,28]{1,0:T(1,128)S(1)}, s32[1,28]{1,0:T(1,128)S(1)}, u32[]{:S(2)}, u32[]{:S(2)}) collective-permute-start(s32[1,28]{1,0:T(1,128)S(1)} %copy-done.17), channel_id=1, source_target_pairs={{0,80},{16,96},{32,112},{48,64},{64,16},{80,32},{96,48},{112,0},{1... | collective-permute-start | bytes 344 | tf_op jit(solution)/shard_map/ppermute | solution.py:240
  39.1 8.0 %collective-permute-start.4 = (s32[1,28]{1,0:T(1,128)S(1)}, s32[1,28]{1,0:T(1,128)S(1)}, u32[]{:S(2)}, u32[]{:S(2)}) collective-permute-start(s32[1,28]{1,0:T(1,128)S(1)} %copy-done.17), channel_id=1, source_target_pairs={{0,112},{16,64},{32,80},{48,96},{64,48},{80,0},{96,16},{112,32},{1... | collective-permute-start | bytes 344 | tf_op jit(solution)/shard_map/ppermute | solution.py:240
  42.7 5.1 %collective-permute-start.5 = (s32[1,28]{1,0:T(1,128)S(1)}, s32[1,28]{1,0:T(1,128)S(1)}, u32[]{:S(2)}, u32[]{:S(2)}) collective-permute-start(s32[1,28]{1,0:T(1,128)S(1)} %copy-done.17), channel_id=1, source_target_pairs={{0,32},{16,48},{32,0},{48,16},{64,96},{80,112},{96,64},{112,80},{1... | collective-permute-start | bytes 344 | tf_op jit(solution)/shard_map/ppermute | solution.py:240
  44.2 6.0 %collective-permute-start.6 = (s32[1,28]{1,0:T(1,128)S(1)}, s32[1,28]{1,0:T(1,128)S(1)}, u32[]{:S(2)}, u32[]{:S(2)}) collective-permute-start(s32[1,28]{1,0:T(1,128)S(1)} %copy-done.17), channel_id=1, source_target_pairs={{0,96},{16,112},{32,64},{48,80},{64,32},{80,48},{96,0},{112,16},{1... | collective-permute-start | bytes 344 | tf_op jit(solution)/shard_map/ppermute | solution.py:240
  47.1 19.1 %collective-permute-start.10 = (bf16[128,2560]{1,0:T(8,128)(2,1)}, bf16[128,2560]{1,0:T(8,128)(2,1)}, u32[]{:S(2)}, u32[]{:S(2)}) collective-permute-start(bf16[128,2560]{1,0:T(8,128)(2,1)} %get-tuple-element.16), channel_id=1, source_target_pairs={{0,16},{16,32},{32,48},{48,0},{1,17},{17,33},{33,49},{49,1},{2,18}... | collective-permute-start | bytes 1966088 | tf_op jit(solution)/shard_map/ppermute | solution.py:224
  47.7 30.3 %collective-permute-start.9 = (bf16[128,2560]{1,0:T(8,128)(2,1)}, bf16[128,2560]{1,0:T(8,128)(2,1)}, u32[]{:S(2)}, u32[]{:S(2)}) collective-permute-start(bf16[128,2560]{1,0:T(8,128)(2,1)} %get-tuple-element.15), channel_id=1, source_target_pairs={{0,16},{16,32},{32,48},{48,0},{1,17},{17,33},{33,49},{49,1},{2,18}... | collective-permute-start | bytes 1966088 | tf_op jit(solution)/shard_map/ppermute | solution.py:224
  50.2 45.5 %collective-permute-start.13 = (bf16[256,2560]{1,0:T(8,128)(2,1)S(1)}, bf16[256,2560]{1,0:T(8,128)(2,1)S(1)}, u32[]{:S(2)}, u32[]{:S(2)}) collective-permute-start(bf16[256,2560]{1,0:T(8,128)(2,1)S(1)} %copy-done), channel_id=1, source_target_pairs={{0,48},{16,0},{32,16},{48,32},{1,49},{17,1},{33,17},{49,33},{2,50}... | collective-permute-start | bytes 3932168 | tf_op jit(solution)/shard_map/ppermute | solution.py:227
  51.5 44.3 %copy-start.4 = (bf16[128,2560]{1,0:T(8,128)(2,1)}, bf16[128,2560]{1,0:T(8,128)(2,1)S(1)}, u32[]{:S(2)}) copy-start(bf16[128,2560]{1,0:T(8,128)(2,1)S(1)} %collective-permute-done.11.refs_3_) | copy-start | bytes 1966084
  51.5 44.9 %collective-permute-start.16 = (bf16[256,2560]{1,0:T(8,128)(2,1)S(1)}, bf16[256,2560]{1,0:T(8,128)(2,1)}, u32[]{:S(2)}, u32[]{:S(2)}) collective-permute-start(bf16[256,2560]{1,0:T(8,128)(2,1)S(1)} %copy-done), channel_id=1, source_target_pairs={{0,64},{64,0},{1,65},{65,1},{2,66},{66,2},{3,67},{67,3},{4,68},{68... | collective-permute-start | bytes 3932168 | tf_op jit(solution)/shard_map/ppermute | solution.py:230
  66.3 27.7 %collective-permute-start.17 = (bf16[128,2560]{1,0:T(8,128)(2,1)S(1)}, bf16[128,2560]{1,0:T(8,128)(2,1)}, u32[]{:S(2)}, u32[]{:S(2)}) collective-permute-start(bf16[128,2560]{1,0:T(8,128)(2,1)S(1)} %copy-done.3), channel_id=1, source_target_pairs={{0,64},{64,0},{1,65},{65,1},{2,66},{66,2},{3,67},{67,3},{4,68},{68... | collective-permute-start | bytes 1966088 | tf_op jit(solution)/shard_map/ppermute | solution.py:230
  78.0 16.2 %collective-permute-start.14 = (bf16[128,2560]{1,0:T(8,128)(2,1)S(1)}, bf16[128,2560]{1,0:T(8,128)(2,1)S(1)}, u32[]{:S(2)}, u32[]{:S(2)}) collective-permute-start(bf16[128,2560]{1,0:T(8,128)(2,1)S(1)} %copy-done.3), channel_id=1, source_target_pairs={{0,48},{16,0},{32,16},{48,32},{1,49},{17,1},{33,17},{49,33},{2,50}... | collective-permute-start | bytes 1966088 | tf_op jit(solution)/shard_map/ppermute | solution.py:227
  94.0 14.2 %collective-permute-start.21 = (bf16[128,2560]{1,0:T(8,128)(2,1)}, bf16[128,2560]{1,0:T(8,128)(2,1)}, u32[]{:S(2)}, u32[]{:S(2)}) collective-permute-start(bf16[128,2560]{1,0:T(8,128)(2,1)} %collective-permute-done.17.refs_2_), channel_id=1, source_target_pairs={{0,16},{16,32},{32,48},{48,0},{1,17},{17,33},{33,49},{49,1},{2,18}... | collective-permute-start | bytes 1966088 | tf_op jit(solution)/shard_map/ppermute | solution.py:224
  94.2 2.1 copy-start.6
  94.2 17.9 %collective-permute-start.19 = (bf16[128,2560]{1,0:T(8,128)(2,1)}, bf16[128,2560]{1,0:T(8,128)(2,1)}, u32[]{:S(2)}, u32[]{:S(2)}) collective-permute-start(bf16[128,2560]{1,0:T(8,128)(2,1)} %collective-permute-done.9.refs_1_), channel_id=1, source_target_pairs={{0,64},{64,0},{1,65},{65,1},{2,66},{66,2},{3,67},{67,3},{4,68},{68... | collective-permute-start | bytes 1966088 | tf_op jit(solution)/shard_map/ppermute | solution.py:230
  95.7 56.6 %copy-start.1 = (bf16[256,2560]{1,0:T(8,128)(2,1)}, bf16[256,2560]{1,0:T(8,128)(2,1)S(1)}, u32[]{:S(2)}) copy-start(bf16[256,2560]{1,0:T(8,128)(2,1)S(1)} %collective-permute-done.13.refs_1_) | copy-start | bytes 3932164
  95.7 30.4 %collective-permute-start.20 = (bf16[128,2560]{1,0:T(8,128)(2,1)}, bf16[128,2560]{1,0:T(8,128)(2,1)S(1)}, u32[]{:S(2)}, u32[]{:S(2)}) collective-permute-start(bf16[128,2560]{1,0:T(8,128)(2,1)} %collective-permute-done.10.refs_2_), channel_id=1, source_target_pairs={{0,64},{64,0},{1,65},{65,1},{2,66},{66,2},{3,67},{67,3},{4,68},{68... | collective-permute-start | bytes 1966088 | tf_op jit(solution)/shard_map/ppermute | solution.py:230
  96.4 31.2 %collective-permute-start.24 = (bf16[128,2560]{1,0:T(8,128)(2,1)}, bf16[128,2560]{1,0:T(8,128)(2,1)}, u32[]{:S(2)}, u32[]{:S(2)}) collective-permute-start(bf16[128,2560]{1,0:T(8,128)(2,1)} %collective-permute-done.17.refs_2_), channel_id=1, source_target_pairs={{0,48},{16,0},{32,16},{48,32},{1,49},{17,1},{33,17},{49,33},{2,50}... | collective-permute-start | bytes 1966088 | tf_op jit(solution)/shard_map/ppermute | solution.py:227
  108.2 69.9 %collective-permute-start.29 = (bf16[256,2560]{1,0:T(8,128)(2,1)S(1)}, bf16[256,2560]{1,0:T(8,128)(2,1)}, u32[]{:S(2)}, u32[]{:S(2)}) collective-permute-start(bf16[256,2560]{1,0:T(8,128)(2,1)S(1)} %collective-permute-done.13.refs_1_), channel_id=1, source_target_pairs={{0,48},{16,0},{32,16},{48,32},{1,49},{17,1},{33,17},{49,33},{2,50}... | collective-permute-start | bytes 3932168 | tf_op jit(solution)/shard_map/ppermute | solution.py:227
  112.2 76.1 %collective-permute-start.23 = (bf16[256,2560]{1,0:T(8,128)(2,1)S(1)}, bf16[256,2560]{1,0:T(8,128)(2,1)S(1)}, u32[]{:S(2)}, u32[]{:S(2)}) collective-permute-start(bf16[256,2560]{1,0:T(8,128)(2,1)S(1)} %collective-permute-done.13.refs_1_), channel_id=1, source_target_pairs={{0,64},{64,0},{1,65},{65,1},{2,66},{66,2},{3,67},{67,3},{4,68},{68... | collective-permute-start | bytes 3932168 | tf_op jit(solution)/shard_map/ppermute | solution.py:230
  126.1 26.2 %copy-start.5 = (bf16[128,2560]{1,0:T(8,128)(2,1)}, bf16[128,2560]{1,0:T(8,128)(2,1)S(1)}, u32[]{:S(2)}) copy-start(bf16[128,2560]{1,0:T(8,128)(2,1)S(1)} %collective-permute-done.20.refs_2_) | copy-start | bytes 1966084
  126.1 19.0 %collective-permute-start.27 = (bf16[128,2560]{1,0:T(8,128)(2,1)}, bf16[128,2560]{1,0:T(8,128)(2,1)S(1)}, u32[]{:S(2)}, u32[]{:S(2)}) collective-permute-start(bf16[128,2560]{1,0:T(8,128)(2,1)} %collective-permute-done.19.refs_1_), channel_id=1, source_target_pairs={{0,16},{16,32},{32,48},{48,0},{1,17},{17,33},{33,49},{49,1},{2,18}... | collective-permute-start | bytes 1966088 | tf_op jit(solution)/shard_map/ppermute | solution.py:224
  127.5 47.5 %collective-permute-start.30 = (bf16[128,2560]{1,0:T(8,128)(2,1)}, bf16[128,2560]{1,0:T(8,128)(2,1)}, u32[]{:S(2)}, u32[]{:S(2)}) collective-permute-start(bf16[128,2560]{1,0:T(8,128)(2,1)} %copy-done.4), channel_id=1, source_target_pairs={{0,16},{16,32},{32,48},{48,0},{1,17},{17,33},{33,49},{49,1},{2,18}... | collective-permute-start | bytes 1966088 | tf_op jit(solution)/shard_map/ppermute | solution.py:224
  145.1 1.8 copy-start.7
  145.1 38.3 %collective-permute-start.26 = (bf16[128,2560]{1,0:T(8,128)(2,1)}, bf16[128,2560]{1,0:T(8,128)(2,1)}, u32[]{:S(2)}, u32[]{:S(2)}) collective-permute-start(bf16[128,2560]{1,0:T(8,128)(2,1)} %collective-permute-done.24.refs_2_), channel_id=1, source_target_pairs={{0,48},{16,0},{32,16},{48,32},{1,49},{17,1},{33,17},{49,33},{2,50}... | collective-permute-start | bytes 1966088 | tf_op jit(solution)/shard_map/ppermute | solution.py:227
  146.9 37.6 %collective-permute-start.25 = (bf16[128,2560]{1,0:T(8,128)(2,1)S(1)}, bf16[128,2560]{1,0:T(8,128)(2,1)}, u32[]{:S(2)}, u32[]{:S(2)}) collective-permute-start(bf16[128,2560]{1,0:T(8,128)(2,1)S(1)} %collective-permute-done.20.refs_2_), channel_id=1, source_target_pairs={{0,16},{16,32},{32,48},{48,0},{1,17},{17,33},{33,49},{49,1},{2,18}... | collective-permute-start | bytes 1966088 | tf_op jit(solution)/shard_map/ppermute | solution.py:224
  169.0 6.0 %copy-start.14 = (f32[1,384]{1,0:T(1,128)S(1)}, f32[1,384]{1,0:T(1,128)}, u32[]{:S(2)}) copy-start(f32[1,384]{1,0:T(1,128)} %score_listed.9) | copy-start | bytes 4612
  169.0 9.1 %copy-start.13 = (f32[1,384]{1,0:T(1,128)S(1)}, f32[1,384]{1,0:T(1,128)}, u32[]{:S(2)}) copy-start(f32[1,384]{1,0:T(1,128)} %score_listed.10) | copy-start | bytes 4612
  175.0 8.5 %copy-start.12 = (f32[1,384]{1,0:T(1,128)S(1)}, f32[1,384]{1,0:T(1,128)}, u32[]{:S(2)}) copy-start(f32[1,384]{1,0:T(1,128)} %score_listed.11) | copy-start | bytes 4612
  175.0 9.5 %copy-start.11 = (f32[1,384]{1,0:T(1,128)S(1)}, f32[1,384]{1,0:T(1,128)}, u32[]{:S(2)}) copy-start(f32[1,384]{1,0:T(1,128)} %score_listed.12) | copy-start | bytes 4612
  175.0 21.6 %collective-permute-start.12 = (f32[1,384]{1,0:T(1,128)S(1)}, f32[1,384]{1,0:T(1,128)S(1)}, u32[]{:S(2)}, u32[]{:S(2)}) collective-permute-start(f32[1,384]{1,0:T(1,128)S(1)} %copy-done.14), channel_id=1, source_target_pairs={{0,48},{16,0},{32,16},{48,32},{64,112},{80,64},{96,80},{112,96},{1... | collective-permute-start | bytes 4616 | tf_op jit(solution)/shard_map/ppermute | solution.py:240
  178.1 18.7 %collective-permute-start.15 = (f32[1,384]{1,0:T(1,128)S(1)}, f32[1,384]{1,0:T(1,128)S(1)}, u32[]{:S(2)}, u32[]{:S(2)}) collective-permute-start(f32[1,384]{1,0:T(1,128)S(1)} %copy-done.13), channel_id=1, source_target_pairs={{0,16},{16,32},{32,48},{48,0},{64,80},{80,96},{96,112},{112,64},{1... | collective-permute-start | bytes 4616 | tf_op jit(solution)/shard_map/ppermute | solution.py:240
  183.5 21.6 %collective-permute-start.18 = (f32[1,384]{1,0:T(1,128)S(1)}, f32[1,384]{1,0:T(1,128)S(1)}, u32[]{:S(2)}, u32[]{:S(2)}) collective-permute-start(f32[1,384]{1,0:T(1,128)S(1)} %copy-done.12), channel_id=1, source_target_pairs={{0,64},{16,80},{32,96},{48,112},{64,0},{80,16},{96,32},{112,48},{1... | collective-permute-start | bytes 4616 | tf_op jit(solution)/shard_map/ppermute | solution.py:240
  184.5 20.6 %collective-permute-start.22 = (f32[1,384]{1,0:T(1,128)S(1)}, f32[1,384]{1,0:T(1,128)S(1)}, u32[]{:S(2)}, u32[]{:S(2)}) collective-permute-start(f32[1,384]{1,0:T(1,128)S(1)} %copy-done.11), channel_id=1, source_target_pairs={{0,112},{16,64},{32,80},{48,96},{64,48},{80,0},{96,16},{112,32},{1... | collective-permute-start | bytes 4616 | tf_op jit(solution)/shard_map/ppermute | solution.py:240
  188.3 1.1 copy-start.2
  188.3 16.9 %collective-permute-start.31 = (f32[1,384]{1,0:T(1,128)}, f32[1,384]{1,0:T(1,128)S(1)}, u32[]{:S(2)}, u32[]{:S(2)}) collective-permute-start(f32[1,384]{1,0:T(1,128)} %score_listed.15), channel_id=1, source_target_pairs={{0,32},{16,48},{32,0},{48,16},{64,96},{80,112},{96,64},{112,80},{1... | collective-permute-start | bytes 4616 | tf_op jit(solution)/shard_map/ppermute | solution.py:240
  196.7 8.5 %collective-permute-start.28 = (f32[1,384]{1,0:T(1,128)}, f32[1,384]{1,0:T(1,128)S(1)}, u32[]{:S(2)}, u32[]{:S(2)}) collective-permute-start(f32[1,384]{1,0:T(1,128)} %get-tuple-element.17), channel_id=1, source_target_pairs={{0,80},{16,96},{32,112},{48,64},{64,16},{80,32},{96,48},{112,0},{1... | collective-permute-start | bytes 4616 | tf_op jit(solution)/shard_map/ppermute | solution.py:240
  196.8 8.4 %copy-start.15 = (f32[1,384]{1,0:T(1,128)S(1)}, f32[1,384]{1,0:T(1,128)}, u32[]{:S(2)}) copy-start(f32[1,384]{1,0:T(1,128)} %get-tuple-element.13) | copy-start | bytes 4612
  196.8 8.4 %copy-start.16 = (f32[1,384]{1,0:T(1,128)S(1)}, f32[1,384]{1,0:T(1,128)}, u32[]{:S(2)}) copy-start(f32[1,384]{1,0:T(1,128)} %get-tuple-element.19) | copy-start | bytes 4612
  196.8 9.1 %copy-start.10 = (f32[384]{0:T(512)S(1)}, f32[384]{0:T(512)}, u32[]{:S(2)}) copy-start(f32[384]{0:T(512)} %param.11) | copy-start | bytes 4612
  196.8 8.4 %collective-permute-start.32 = (f32[1,384]{1,0:T(1,128)}, f32[1,384]{1,0:T(1,128)S(1)}, u32[]{:S(2)}, u32[]{:S(2)}) collective-permute-start(f32[1,384]{1,0:T(1,128)} %get-tuple-element.18), channel_id=1, source_target_pairs={{0,96},{16,112},{32,64},{48,80},{64,32},{80,48},{96,0},{112,16},{1... | collective-permute-start | bytes 4616 | tf_op jit(solution)/shard_map/ppermute | solution.py:240
  205.9 22.8 %copy-start.8 = (f32[384]{0:T(512)}, f32[384]{0:T(512)S(1)}, u32[]{:S(2)}) copy-start(f32[384]{0:T(512)S(1)} %subtract_reduce_fusion) | copy-start | bytes 4612

commit v2 on v1

v2 whole, which is shorter than its diff:
```python
import jax
import jax.numpy as jnp
from jax import lax
from jax.experimental import pallas as pl
from jax.experimental.pallas import tpu as pltpu
from jax.sharding import Mesh
from jax.sharding import PartitionSpec as P


RING = "grp_1"
CORE = "grp_2"
PLANE = ("grp_0", "grp_1")
GRP_REP = ("grp_0", "grp_1", "grp_2", "rep_0", "rep_1")

inverse_softmax_sharpness = 20.0
norm_epsilon = 1e-06
LOCAL_BLOCKS = 2
PIECES = 3
EXTRA = 16
LOCAL_LIMIT = 56
SLOTS = 2

NT = (((1,), (1,)), ((), ()))


def normalize(rows):
    values = rows.astype(jnp.float32)
    scale = lax.rsqrt(jnp.sum(values * values, axis=-1, keepdims=True) + norm_epsilon)
    return (values * scale).astype(jnp.bfloat16)


def units_kernel(queries, *pieces):
    at = 0
    for piece in pieces:
        rows = piece.shape[0]
        piece[...] = normalize(queries[at : at + rows, :])
        at += rows


def query_units(queries, start, sizes):
    width = queries.shape[1]
    rows = sum(sizes)
    return pl.pallas_call(
        units_kernel,
        grid=(1,),
        in_specs=[pl.BlockSpec((rows, width), lambda i: (start // rows, 0))],
        out_specs=[pl.BlockSpec((n, width), lambda i: (0, 0)) for n in sizes],
        out_shape=[jax.ShapeDtypeStruct((n, width), jnp.bfloat16) for n in sizes],
        cost_estimate=pl.CostEstimate(
            flops=3 * rows * width, transcendentals=rows, bytes_accessed=4 * rows * width
        ),
        compiler_params=pltpu.CompilerParams(vmem_limit_bytes=12 * 2**20),
    )(queries)


def local_kernel(counts, a, b, c, positive, passages, units, total, score, questions):
    step = pl.program_id(0)
    rows = passages.shape[0]
    block_rows = rows // LOCAL_BLOCKS

    @pl.when(step == 0)
    def _():
        at = 0
        for piece in (a, b, c):
            questions[at : at + piece.shape[0], :] = piece[...]
            at += piece.shape[0]
        total[...] = jnp.zeros_like(total)
        score[...] = jnp.zeros_like(score)

    units[...] = normalize(passages[...])
    similarity = (
        lax.dot_general(units[...], questions[...], NT, preferred_element_type=jnp.float32)
        * inverse_softmax_sharpness
    )
    row = lax.broadcasted_iota(jnp.int32, similarity.shape, 0)
    score[...] += jnp.sum(
        jnp.where(row + step * rows == positive[...], similarity, 0.0), axis=0, keepdims=True
    )
    kept = jnp.exp(similarity)
    for k in range(LOCAL_BLOCKS):
        part = slice(k * block_rows, (k + 1) * block_rows)
        inside = row[:block_rows] < counts[step * LOCAL_BLOCKS + k]
        total[...] += jnp.sum(jnp.where(inside, kept[part], 0.0), axis=0, keepdims=True)


def score_local(counts, pieces, positive, passages):
    local_rows, width = passages.shape
    blocks = counts.shape[0]
    step_rows = local_rows // blocks * LOCAL_BLOCKS
    steps = blocks // LOCAL_BLOCKS
    rows = positive.shape[1]
    piece = lambda a: pl.BlockSpec(a.shape, lambda s, c: (0, 0))
    line = pl.BlockSpec((1, rows), lambda s, c: (0, 0))
    band = pl.BlockSpec((step_rows, width), lambda s, c: (s, 0))
    return pl.pallas_call(
        local_kernel,
        grid_spec=pltpu.PrefetchScalarGridSpec(
            num_scalar_prefetch=1,
            grid=(steps,),
            in_specs=[piece(a) for a in pieces] + [line, band],
            out_specs=[band, line, line],
            scratch_shapes=[pltpu.VMEM((rows, width), jnp.bfloat16)],
        ),
        out_shape=[
            jax.ShapeDtypeStruct(passages.shape, jnp.bfloat16),
            jax.ShapeDtypeStruct((1, rows), jnp.float32),
            jax.ShapeDtypeStruct((1, rows), jnp.float32),
        ],
        cost_estimate=pl.CostEstimate(
            flops=2 * local_rows * width * rows,
            transcendentals=local_rows * rows,
            bytes_accessed=4 * local_rows * width,
        ),
        compiler_params=pltpu.CompilerParams(vmem_limit_bytes=LOCAL_LIMIT * 2**20),
        name="local",
    )(counts, *pieces, positive, passages)


def listed_kernel(jobs, table, *refs):
    refs = list(refs)
    take = lambda n: [refs.pop(0) for _ in range(n)]
    pieces = [take(count) for _, _, count, _, _ in jobs]
    given = [take(1)[0] if is_given else None for _, _, _, is_given, _ in jobs]
    mine, twin = (None, None) if all(job[3] for job in jobs) else take(2)
    totals = [take(1)[0] if count else None for _, _, count, _, _ in jobs]
    held = [take(1)[0] if keep else None for _, _, _, _, keep in jobs]
    held = [ref if job[4] or job[3] else take(1)[0] for ref, job in zip(held, jobs)]
    stacks = [take(1)[0] if count else None for _, _, count, _, _ in jobs]
    (sems,) = refs

    started = []
    for j, (source, slots, _, is_given, _) in enumerate(jobs):
        group = []
        at = 0
        for k, piece in enumerate(pieces[j]):
            target = stacks[j].at[pl.ds(at, piece.shape[0])]
            group.append(pltpu.make_async_copy(piece, target, sems.at[j, 2 * SLOTS + k]))
            at += piece.shape[0]
        for k, s in enumerate(() if is_given else slots):
            home = mine if s < SLOTS else twin
            block = home.at[table[source * 4 * SLOTS + s]]
            target = held[j].at[pl.ds(k * mine.shape[1], mine.shape[1])]
            group.append(pltpu.make_async_copy(block, target, sems.at[j, k]))
        for copy in group:
            copy.start()
        started.append(group)
    for j, (source, slots, count, is_given, _) in enumerate(jobs):
        for copy in started[j]:
            copy.wait()
        if not count:
            continue
        keys = given[j] if is_given else held[j]
        block_rows = keys.shape[0] // len(slots)
        similarity = (
            lax.dot_general(keys[...], stacks[j][...], NT, preferred_element_type=jnp.float32)
            * inverse_softmax_sharpness
        )
        kept = jnp.exp(similarity)
        row = lax.broadcasted_iota(jnp.int32, (block_rows, kept.shape[1]), 0)
        total = jnp.zeros((1, kept.shape[1]), jnp.float32)
        for k, s in enumerate(slots):
            inside = row < table[source * 4 * SLOTS + 2 * SLOTS + s]
            part = kept[k * block_rows : (k + 1) * block_rows]
            total += jnp.sum(jnp.where(inside, part, 0.0), axis=0, keepdims=True)
        totals[j][...] = total


def score_listed(table, mine, twin, rows, jobs, limit):
    width = mine.shape[2]
    block_rows = mine.shape[1]
    plan, operands = [], []
    for source, pieces, given, keep in jobs:
        slots = tuple(range(SLOTS if source == 0 else 0, 2 * SLOTS))
        plan.append((source, slots, len(pieces), given is not None, keep))
        operands += pieces
    scored = sum(job[2] > 0 for job in plan)
    given = [keys for _, _, keys, _ in jobs if keys is not None]
    held = lambda job: (len(job[1]) * block_rows, width)
    outs = [jax.ShapeDtypeStruct((1, rows), jnp.float32)] * scored
    outs += [jax.ShapeDtypeStruct(held(job), jnp.bfloat16) for job in plan if job[4]]
    scratch = [pltpu.VMEM(held(job), jnp.bfloat16) for job in plan if not (job[3] or job[4])]
    scratch += [pltpu.VMEM((rows, width), jnp.bfloat16)] * scored
    sources = [] if all(job[3] for job in plan) else [mine, twin]
    vmem = pl.BlockSpec(memory_space=pltpu.VMEM)
    hbm = pl.BlockSpec(memory_space=pltpu.HBM)
    kernel = lambda *refs: listed_kernel(plan, *refs)
    return pl.pallas_call(
        kernel,
        in_specs=[pl.BlockSpec(memory_space=pltpu.SMEM)]
        + [hbm] * len(operands)
        + [vmem] * len(given)
        + [hbm] * len(sources),
        out_specs=[vmem] * len(outs),
        out_shape=outs,
        scratch_shapes=scratch + [pltpu.SemaphoreType.DMA((len(plan), 2 * SLOTS + PIECES))],
        cost_estimate=pl.CostEstimate(
            flops=4 * SLOTS * block_rows * width * rows * scored,
            transcendentals=2 * SLOTS * block_rows * rows * scored,
            bytes_accessed=(2 * SLOTS * block_rows * len(jobs) + rows * scored) * width * 2,
        ),
        compiler_params=pltpu.CompilerParams(vmem_limit_bytes=limit * 2**20),
        name="listed",
    )(table, *operands, *given, *sources)


def last_kernel(source, count, table, *refs):
    pieces, (keys, base, *parts) = refs[:count], refs[count:-4]
    loss, shares, stack, _ = refs[-4:]
    at = 0
    for piece in pieces:
        stack[at : at + piece.shape[0], :] = piece[...]
        at += piece.shape[0]
    total = base[0:1, :]
    for part in parts:
        total += part[...]
    similarity = (
        lax.dot_general(keys[...], stack[...], NT, preferred_element_type=jnp.float32)
        * inverse_softmax_sharpness
    )
    kept = jnp.exp(similarity)
    block_rows = keys.shape[0] // (2 * SLOTS)
    row = lax.broadcasted_iota(jnp.int32, (block_rows, kept.shape[1]), 0)
    for s in range(2 * SLOTS):
        inside = row < table[source * 4 * SLOTS + 2 * SLOTS + s]
        part = kept[s * block_rows : (s + 1) * block_rows]
        total += jnp.sum(jnp.where(inside, part, 0.0), axis=0, keepdims=True)
    value = jnp.log(total) - base[1:2, :]
    loss[...] = value
    weights = base[2:3, :]
    lane = lax.broadcasted_iota(jnp.int32, shares.shape, 1)
    weighted = jnp.sum(weights * value, axis=1, keepdims=True)
    weight = jnp.sum(weights, axis=1, keepdims=True)
    shares[...] = jnp.where(lane == 0, weighted, weight)


def score_last(table, source, pieces, keys, base, parts, everyone):
    rows = base.shape[1]
    width = keys.shape[1]
    vmem = pl.BlockSpec(memory_space=pltpu.VMEM)
    hbm = pl.BlockSpec(memory_space=pltpu.HBM)
    kernel = lambda *refs: last_kernel(source, len(pieces), *refs)
    return pl.pallas_call(
        kernel,
        in_specs=[pl.BlockSpec(memory_space=pltpu.SMEM)]
        + [vmem] * len(pieces)
        + [vmem] * (2 + len(parts)),
        out_specs=[vmem, vmem],
        out_shape=[
            jax.ShapeDtypeStruct((1, rows), jnp.float32),
            jax.ShapeDtypeStruct((everyone, 2), jnp.float32),
        ],
        scratch_shapes=[
            pltpu.VMEM((rows, width), jnp.bfloat16),
            pltpu.SemaphoreType.DMA((len(pieces),)),
        ],
        cost_estimate=pl.CostEstimate(
            flops=2 * keys.shape[0] * width * rows,
            transcendentals=keys.shape[0] * rows,
            bytes_accessed=2 * (keys.shape[0] + rows) * width,
        ),
        compiler_params=pltpu.CompilerParams(vmem_limit_bytes=12 * 2**20),
        name="last",
    )(table, *pieces, keys, base, *parts)


def slot_table(lists, device, blocks_here, counts):
    owner = lists // blocks_here
    block = lists % blocks_here
    mine = owner == device
    first = jnp.max(jnp.where(mine, block, -1), axis=1)
    second = jnp.min(jnp.where(mine, block, blocks_here), axis=1)
    second = jnp.where(jnp.sum(mine, axis=1) > 1, second, -1)
    index = jnp.stack([first, second], axis=1)
    choice = index[:, :, None] == jnp.arange(blocks_here, dtype=jnp.int32)[None, None, :]
    kept = jnp.sum(jnp.where(choice, counts[None, None, :], 0), axis=2)
    return jnp.maximum(index, 0), kept


def local(queries, passages, block_valid_counts, positive_index, neg_blocks, query_weights):
    rows, width = queries.shape
    blocks_here = block_valid_counts.shape[0]
    ring = lax.axis_size(RING)
    replicas = lax.axis_size("rep_0") * lax.axis_size("rep_1")
    device = lax.axis_index(GRP_REP)

    def shift(a, dx, dz):
        pairs = []
        for i in range(2 * ring):
            x, z = divmod(i, ring)
            pairs.append((i, (x ^ dx) * ring + (z + dz) % ring))
        return lax.ppermute(a, PLANE, pairs)

    forward = lambda a: shift(a, 0, 1)
    backward = lambda a: shift(a, 0, -1)
    across = lambda a: shift(a, 1, 0)

    def swap(a):
        return lax.ppermute(a, CORE, [(0, 1), (1, 0)])

    pair = jnp.concatenate([neg_blocks, across(neg_blocks)], axis=0)
    rows_c = rows // PIECES
    rows_a = rows_c + EXTRA
    (c,) = query_units(queries[rows - rows_c :], 0, [rows_c])
    a, b = query_units(queries, 0, [rows_a, rows - rows_c - rows_a])
    beside_c = across(c)
    below_c = forward(c)
    above_c = backward(c)
    pair_below = forward(pair)
    pair_above = backward(pair)
    beside_b = across(b)
    below_a = forward(a)
    above_a = backward(a)
    beside_a = across(a)
    below_b = forward(b)
    above_b = backward(b)
    twin_counts = swap(block_valid_counts)
    pair_facing = forward(pair_below)

    beside_below_c = forward(beside_c)
    facing_c = backward(above_c)
    beside_below_a = across(below_a)
    facing_a = forward(below_a)
    beside_above_b = backward(beside_b)
    beside_below_b = across(below_b)
    beside_above_c = across(above_c)
    facing_b = forward(below_b)
    beside_above_a = backward(beside_a)
    beside_facing_c = forward(beside_below_c)
    beside_facing_a = across(facing_a)
    beside_facing_b = backward(beside_above_b)

    positive = positive_index[None, :]
    units, local_total, positive_score = score_local(
        block_valid_counts, (a, b, c), positive, passages
    )
    blocks = units.reshape(blocks_here, -1, width)
    twin = swap(blocks)

    def slots(lists):
        listed = jnp.concatenate(lists, axis=0)
        index_mine, kept_mine = slot_table(listed, device, blocks_here, block_valid_counts)
        index_twin, kept_twin = slot_table(listed, device ^ replicas, blocks_here, twin_counts)
        return jnp.concatenate([index_mine, index_twin, kept_mine, kept_twin], axis=1).reshape(-1)

    near_table = slots([pair, pair_below, pair_above])
    table = jnp.concatenate([near_table, slots([pair_facing])])

    def score(table, jobs, limit):
        return score_listed(table, blocks, twin, rows, jobs, limit)

    own_total, beside_total, below_total, above_total = score(
        near_table,
        [
            (0, [a, b, c], None, False),
            (1, [beside_a, beside_b, beside_c], None, False),
            (2, [below_a, below_b, below_c], None, False),
            (4, [above_a, above_b, above_c], None, False),
        ],
        56,
    )
    beside_below_total, keys = score(
        table,
        [
            (3, [beside_below_a, beside_below_b, beside_below_c], None, False),
            (7, [], None, True),
        ],
        56,
    )
    facing_total, beside_above_total = score(
        table,
        [
            (6, [facing_a, facing_b, facing_c], None, False),
            (5, [beside_above_a, beside_above_b, beside_above_c], None, False),
        ],
        56,
    )
    half = ring // 2
    base = jnp.concatenate([local_total + own_total, positive_score, query_weights[None, :]])
    base = shift(base, 1, half)
    parts = [
        shift(beside_total, 0, half),
        shift(below_total, 1, half - 1),
        shift(above_total, 1, half + 1),
        shift(beside_below_total, 0, half - 1),
        shift(facing_total, 1, 0),
        shift(beside_above_total, 0, half + 1),
    ]
    query_loss, shares = score_last(
        table,
        7,
        [beside_facing_a, beside_facing_b, beside_facing_c],
        keys,
        base,
        parts,
        lax.axis_size(GRP_REP),
    )
    query_loss = shift(query_loss[0], 1, half)
    shares = lax.all_to_all(shares, GRP_REP, split_axis=0, concat_axis=0, tiled=True)
    sums = jnp.sum(shares, axis=0)
    return (query_loss, sums[0] / sums[1])


def solution(mesh):
    split = Mesh(mesh.devices.reshape(2, 4, 2, 4, 2), GRP_REP)
    in_specs = (
        P(GRP_REP, None),
        P(GRP_REP, None),
        P(GRP_REP),
        P(GRP_REP),
        P(GRP_REP, None),
        P(GRP_REP),
    )
    out_specs = (P(GRP_REP), P())

    return jax.shard_map(local, mesh=split, in_specs=in_specs, out_specs=out_specs, check_vma=False)
```

time: 231 us -> 210 us (0.909)
  Pallas kernels: 62.6 us -> 39.8 us
  blocking collectives: 18.8 us -> 0 us
  starting transfers between devices: 41.6 us -> 57.7 us
  local copies, waits for them, and re-layouts: 3.04 us -> 11 us
  waiting for transfers between devices: 97 us -> 94.3 us
    pallas_call x8 -> x3, Pallas kernels: 44.9 us -> 22.4 us  [score_listed(): pl.pallas_call(kernel, in_specs=[pl.BlockSpec(memory_space=pltpu.SMEM)] +...]
    all_to_all x1 -> x0, blocking collectives: 18.8 us -> none  [local(): lax.all_to_all(jnp.broadcast_to(sums[None, :], (everyone, 2)), GRP_REP, s...]
    ppermute x2, waiting for transfers between devices: 11 us -> 0.01 us  [swap(): return lax.ppermute(a, CORE, [(0, 1), (1, 0)])]
    ppermute x31 -> x33, starting transfers between devices: 41.4 us -> 49.9 us  [shift(): return lax.ppermute(a, PLANE, pairs)]
    all_to_all x0 -> x1, starting transfers between devices: none -> 7.77 us  [local(): lax.all_to_all(shares, GRP_REP, split_axis=0, concat_axis=0, tiled=True)]
    unnamed x38 -> x53, local copies, waits for them, and re-layouts: 1.15 us -> 7.06 us
    all_to_all x0 -> x1, waiting for transfers between devices: none -> 5.56 us  [local(): lax.all_to_all(shares, GRP_REP, split_axis=0, concat_axis=0, tiled=True)]
    ppermute x31 -> x33, waiting for transfers between devices: 86 us -> 88.8 us  [shift(): return lax.ppermute(a, PLANE, pairs)]
  transfers between devices with their start and end apart: 33 -> 36, of which waited for: 12 -> 14; matrix products, arithmetic and copies ran while one was open for 1% -> 2% of each run, Pallas kernels for 20% -> 11%
where the time goes in v2:
time: 210 us; the launch traced here: 209 us
  waiting for transfers between devices  94.3 us (45%)
  starting transfers between devices  57.7 us (27%)
  Pallas kernels  39.8 us (19%)
  local copies, waits for them, and re-layouts  11 us (5%)
  between operations  3.49 us (2%)
  other arithmetic  3.01 us (1%)
    ppermute x33, waiting for transfers between devices, shift(): return lax.ppermute(a, PLANE, pairs)  88.8 us
    ppermute x33, starting transfers between devices, shift(): return lax.ppermute(a, PLANE, pairs)  49.9 us
    pallas_call x3, Pallas kernels, score_listed(): pl.pallas_call(kernel, in_specs=[pl.BlockSpec(memory_space=pltpu.SMEM)] +...  22.4 us
    pallas_call x1, Pallas kernels, score_local(): pl.pallas_call(local_kernel, grid_spec=pltpu.PrefetchScalarGridSpec(num_s...  13.9 us
    all_to_all x1, starting transfers between devices, local(): lax.all_to_all(shares, GRP_REP, split_axis=0, concat_axis=0, tiled=True)  7.77 us
    unnamed x53, local copies, waits for them, and re-layouts  7.06 us
    all_to_all x1, waiting for transfers between devices, local(): lax.all_to_all(shares, GRP_REP, split_axis=0, concat_axis=0, tiled=True)  5.56 us
  transfers between devices with their start and end apart: 36, of which 14 were waited for; matrix products, arithmetic and copies ran while one was open for 2% of the time, Pallas kernels for 11%

profile of v2, /device:TPU:0, one launch (start us, length us, event | category | flops | bytes accessed | tf_op | source)
XLA Modules:
  0.0 209.3 jit_solution(18366421912674175479)
XLA Ops:
  0.6 1.5 copy-done
  2.2 0.4 shard_map.77
  2.6 0.9 copy-done.4
  3.5 1.3 slice.9.queries
  4.8 0.2 shard_map.78.c.refs_3_
  5.1 0.8 copy-done.2
  5.9 1.2 broadcast_in_dim.82.positive
  7.2 13.9 %local.1 = (bf16[2048,2560]{1,0:T(8,128)(2,1)}, f32[1,384]{1,0:T(1,128)}, f32[1,384]{1,0:T(1,128)}) custom-call(s32[16]{0:T(128)} %counts.1, bf16[144,2560]{1,0:T(8,128)(2,1)} %copy-done.4, bf16[112,2560]{1,0:T(8,128)(2,1)} %copy-done.6, bf16[128,2560]{1,0:T(8,128)(2,1)} %copy-done.2, s32[1,384]{1,0:T(1,128)} %broadcast_in_dim.82.positive, ...), custom_call_target="tpu_custom_call" | custom-call | flops 4026531840 | bytes 20971520 | tf_op jit(solution)/shard_map/local/pallas_call | solution.py:95
  21.1 2.1 collective-permute-start.15
  23.2 1.5 collective-permute-start.8
  24.7 0.5 collective-permute-start
  25.3 13.1 %collective-permute-done = s32[1,28]{1,0:T(1,128)S(1)} collective-permute-done((s32[1,28]{1,0:T(1,128)S(1)}, s32[1,28]{1,0:T(1,128)S(1)}, u32[]{:S(2)}, u32[]{:S(2)}) %collective-permute-start) | collective-permute-done | bytes 144 | tf_op jit(solution)/shard_map/ppermute | solution.py:291
  38.4 2.4 %collective-permute-start.21 = (bf16[112,2560]{1,0:T(8,128)(2,1)S(1)}, bf16[112,2560]{1,0:T(8,128)(2,1)S(1)}, u32[]{:S(2)}, u32[]{:S(2)}) collective-permute-start(bf16[112,2560]{1,0:T(8,128)(2,1)S(1)} %copy-done.7), channel_id=1, source_target_pairs={{0,48},{16,0},{32,16},{48,32},{64,112},{80,64},{96,80},{112,96},{1... | collective-permute-start | bytes 1720328 | tf_op jit(solution)/shard_map/ppermute | solution.py:291
  40.9 4.8 %collective-permute-done.1 = s32[2,28]{1,0:T(2,128)S(1)} collective-permute-done((s32[2,28]{1,0:T(2,128)S(1)}, s32[2,28]{1,0:T(2,128)S(1)}, u32[]{:S(2)}, u32[]{:S(2)}) %collective-permute-start.1) | collective-permute-done | bytes 256 | tf_op jit(solution)/shard_map/ppermute | solution.py:291
  45.6 0.5 collective-permute-start.2
  46.2 6.6 %collective-permute-done.2 = s32[2,28]{1,0:T(2,128)S(1)} collective-permute-done((s32[2,28]{1,0:T(2,128)S(1)}, s32[2,28]{1,0:T(2,128)S(1)}, u32[]{:S(2)}, u32[]{:S(2)}) %collective-permute-start.2) | collective-permute-done | bytes 256 | tf_op jit(solution)/shard_map/ppermute | solution.py:291
  52.8 1.7 collective-permute-start.4
  54.5 3.4 %collective-permute-done.4 = s32[2,28]{1,0:T(2,128)S(1)} collective-permute-done((s32[2,28]{1,0:T(2,128)S(1)}, s32[2,28]{1,0:T(2,128)S(1)}, u32[]{:S(2)}, u32[]{:S(2)}) %collective-permute-start.4) | collective-permute-done | bytes 256 | tf_op jit(solution)/shard_map/ppermute | solution.py:291
  58.0 2.0 collective-permute-start.22
  60.0 0.2 select_reduce_fusion.3
  60.3 1.6 collective-permute-start.11
  61.9 0.1 collective-permute-start.19
  62.1 0.6 copy-done.15
  62.7 9.7 %collective-permute-done.22.refs_12_ = bf16[128,2560]{1,0:T(8,128)(2,1)} collective-permute-done((bf16[128,2560]{1,0:T(8,128)(2,1)S(1)}, bf16[128,2560]{1,0:T(8,128)(2,1)}, u32[]{:S(2)}, u32[]{:S(2)}) %collective-permute-start.22) | collective-permute-done | bytes 655392 | tf_op jit(solution)/shard_map/ppermute | solution.py:291
  72.4 1.5 collective-permute-start.18
  74.0 2.6 %collective-permute-done.11.refs_6_ = bf16[128,2560]{1,0:T(8,128)(2,1)} collective-permute-done((bf16[128,2560]{1,0:T(8,128)(2,1)S(1)}, bf16[128,2560]{1,0:T(8,128)(2,1)}, u32[]{:S(2)}, u32[]{:S(2)}) %collective-permute-start.11) | collective-permute-done | bytes 655392 | tf_op jit(solution)/shard_map/ppermute | solution.py:291
  76.6 3.0 %collective-permute-start.20 = (bf16[144,2560]{1,0:T(8,128)(2,1)S(1)}, bf16[144,2560]{1,0:T(8,128)(2,1)}, u32[]{:S(2)}, u32[]{:S(2)}) collective-permute-start(bf16[144,2560]{1,0:T(8,128)(2,1)S(1)} %copy-done.5), channel_id=1, source_target_pairs={{0,48},{16,0},{32,16},{48,32},{64,112},{80,64},{96,80},{112,96},{1... | collective-permute-start | bytes 2211848 | tf_op jit(solution)/shard_map/ppermute | solution.py:291
  79.7 11.5 %collective-permute-done.19.refs_9_ = bf16[128,2560]{1,0:T(8,128)(2,1)} collective-permute-done((bf16[128,2560]{1,0:T(8,128)(2,1)S(1)}, bf16[128,2560]{1,0:T(8,128)(2,1)}, u32[]{:S(2)}, u32[]{:S(2)}) %collective-permute-start.19) | collective-permute-done | bytes 655392 | tf_op jit(solution)/shard_map/ppermute | solution.py:291
  91.2 3.2 %collective-permute-start.9 = (bf16[112,2560]{1,0:T(8,128)(2,1)}, bf16[112,2560]{1,0:T(8,128)(2,1)}, u32[]{:S(2)}, u32[]{:S(2)}) collective-permute-start(bf16[112,2560]{1,0:T(8,128)(2,1)} %collective-permute-done.8.refs_5_), channel_id=1, source_target_pairs={{0,48},{16,0},{32,16},{48,32},{64,112},{80,64},{96,80},{112,96},{1... | collective-permute-start | bytes 1720328 | tf_op jit(solution)/shard_map/ppermute | solution.py:291
  94.5 0.2 fusion
  94.7 0.2 fusion.1
  95.2 0.2 select_reduce_fusion.7
  95.4 1.6 collective-permute-start.31
  97.0 7.6 %collective-permute-done.28.refs_2_ = bf16[112,2560]{1,0:T(8,128)(2,1)S(1)} collective-permute-done((bf16[112,2560]{1,0:T(8,128)(2,1)}, bf16[112,2560]{1,0:T(8,128)(2,1)S(1)}, u32[]{:S(2)}, u32[]{:S(2)}) %collective-permute-start.28) | collective-permute-done | bytes 573472 | tf_op jit(solution)/shard_map/ppermute | solution.py:291
  104.6 0.8 copy-done.16
  105.4 2.8 %collective-permute-done.9.refs_5_ = bf16[112,2560]{1,0:T(8,128)(2,1)} collective-permute-done((bf16[112,2560]{1,0:T(8,128)(2,1)}, bf16[112,2560]{1,0:T(8,128)(2,1)}, u32[]{:S(2)}, u32[]{:S(2)}) %collective-permute-start.9) | collective-permute-done | bytes 573472 | tf_op jit(solution)/shard_map/ppermute | solution.py:291
  108.1 3.7 %collective-permute-start.30 = (bf16[144,2560]{1,0:T(8,128)(2,1)S(1)}, bf16[144,2560]{1,0:T(8,128)(2,1)S(1)}, u32[]{:S(2)}, u32[]{:S(2)}) collective-permute-start(bf16[144,2560]{1,0:T(8,128)(2,1)S(1)} %collective-permute-done.18.refs_4_), channel_id=1, source_target_pairs={{0,48},{16,0},{32,16},{48,32},{64,112},{80,64},{96,80},{112,96},{1... | collective-permute-start | bytes 2211848 | tf_op jit(solution)/shard_map/ppermute | solution.py:291
  111.8 10.3 %collective-permute-done.29.refs_3_ = bf16[128,2560]{1,0:T(8,128)(2,1)} collective-permute-done((bf16[128,2560]{1,0:T(8,128)(2,1)}, bf16[128,2560]{1,0:T(8,128)(2,1)}, u32[]{:S(2)}, u32[]{:S(2)}) %collective-permute-start.29) | collective-permute-done | bytes 655392 | tf_op jit(solution)/shard_map/ppermute | solution.py:291
  122.6 0.2 fusion.3
  122.8 0.2 fusion.4
  123.2 1.5 collective-permute-start.14
  124.7 0.6 pad_add_fusion.8.refs_0_
  125.3 11.3 %collective-permute-done.12.refs_3_ = bf16[128,2560]{1,0:T(8,128)(2,1)} collective-permute-done((bf16[128,2560]{1,0:T(8,128)(2,1)}, bf16[128,2560]{1,0:T(8,128)(2,1)}, u32[]{:S(2)}, u32[]{:S(2)}) %collective-permute-start.12) | collective-permute-done | bytes 655392 | tf_op jit(solution)/shard_map/ppermute | solution.py:291
  136.6 1.5 collective-permute-start.16
  138.0 2.3 %collective-permute-start.10 = (bf16[112,2560]{1,0:T(8,128)(2,1)}, bf16[112,2560]{1,0:T(8,128)(2,1)S(1)}, u32[]{:S(2)}, u32[]{:S(2)}) collective-permute-start(bf16[112,2560]{1,0:T(8,128)(2,1)} %collective-permute-done.9.refs_5_), channel_id=1, source_target_pairs={{0,48},{16,0},{32,16},{48,32},{64,112},{80,64},{96,80},{112,96},{1... | collective-permute-start | bytes 1720328 | tf_op jit(solution)/shard_map/ppermute | solution.py:291
  140.4 0.8 collective-permute-start.7
  141.2 9.4 %listed.4 = (f32[1,384]{1,0:T(1,128)}, f32[1,384]{1,0:T(1,128)}, f32[1,384]{1,0:T(1,128)}, f32[1,384]{1,0:T(1,128)}) custom-call(s32[48]{0:T(128)} %copy-done.20, bf16[144,2560]{1,0:T(8,128)(2,1)} %copy-done.4, bf16[112,2560]{1,0:T(8,128)(2,1)} %copy-done.6, bf16[128,2560]{1,0:T(8,128)(2,1)} %copy-done.2, bf16[144,2560]{1,0:T(8,128)(2,1)} %copy-done.11, ...), custom_call_target="tpu_custom_call" | custom-call | flops 4026531840 | bytes 18350080 | tf_op jit(solution)/shard_map/listed/pallas_call | solution.py:187
  150.7 0.7 add.39
  151.4 6.8 %listed.5 = (f32[1,384]{1,0:T(1,128)}, f32[1,384]{1,0:T(1,128)}) custom-call(s32[64]{0:T(128)} %pad_add_fusion.8.refs_0_, bf16[144,2560]{1,0:T(8,128)(2,1)} %copy-done.12, bf16[112,2560]{1,0:T(8,128)(2,1)} %copy-done.16, bf16[128,2560]{1,0:T(8,128)(2,1)} %collective-permute-done.29.refs_3_, bf16[144,2560]{1,0:T(8,128)(2,1)} %copy-done.13, ...), custom_call_target="tpu_custom_call" | custom-call | flops 2013265920 | bytes 9175040 | tf_op jit(solution)/shard_map/listed/pallas_call | solution.py:187
  158.2 2.8 %collective-permute-start.32 = (f32[1,384]{1,0:T(1,128)}, f32[1,384]{1,0:T(1,128)S(1)}, u32[]{:S(2)}, u32[]{:S(2)}) collective-permute-start(f32[1,384]{1,0:T(1,128)} %get-tuple-element.28), channel_id=1, source_target_pairs={{0,64},{16,80},{32,96},{48,112},{64,0},{80,16},{96,32},{112,48},{1... | collective-permute-start | bytes 4616 | tf_op jit(solution)/shard_map/ppermute | solution.py:291
  161.0 4.2 %collective-permute-start.33 = (f32[1,384]{1,0:T(1,128)}, f32[1,384]{1,0:T(1,128)S(1)}, u32[]{:S(2)}, u32[]{:S(2)}) collective-permute-start(f32[1,384]{1,0:T(1,128)} %get-tuple-element.29), channel_id=1, source_target_pairs={{0,48},{16,0},{32,16},{48,32},{64,112},{80,64},{96,80},{112,96},{1... | collective-permute-start | bytes 4616 | tf_op jit(solution)/shard_map/ppermute | solution.py:291
  165.3 6.1 %listed.3 = (f32[1,384]{1,0:T(1,128)}, bf16[512,2560]{1,0:T(8,128)(2,1)}) custom-call(s32[64]{0:T(128)} %pad_add_fusion.8.refs_0_, bf16[144,2560]{1,0:T(8,128)(2,1)} %copy-done.9, bf16[112,2560]{1,0:T(8,128)(2,1)} %copy-done.14, bf16[128,2560]{1,0:T(8,128)(2,1)} %collective-permute-done.12.refs_3_, bf16[16,128,2560]{2,1,0:T(8,128)(2,1)} %bitcast.20, ...), custom_call_target="tpu_custom_call" | custom-call | flops 1006632960 | bytes 7208960 | tf_op jit(solution)/shard_map/listed/pallas_call | solution.py:187
  171.4 3.1 %collective-permute-start.24 = (f32[1,384]{1,0:T(1,128)S(1)}, f32[1,384]{1,0:T(1,128)S(1)}, u32[]{:S(2)}, u32[]{:S(2)}) collective-permute-start(f32[1,384]{1,0:T(1,128)S(1)} %copy-done.25), channel_id=1, source_target_pairs={{0,32},{16,48},{32,0},{48,16},{64,96},{80,112},{96,64},{112,80},{1... | collective-permute-start | bytes 4616 | tf_op jit(solution)/shard_map/ppermute | solution.py:291
  174.5 4.1 %collective-permute-start.26 = (f32[1,384]{1,0:T(1,128)S(1)}, f32[1,384]{1,0:T(1,128)S(1)}, u32[]{:S(2)}, u32[]{:S(2)}) collective-permute-start(f32[1,384]{1,0:T(1,128)S(1)} %copy-done.23), channel_id=1, source_target_pairs={{0,112},{16,64},{32,80},{48,96},{64,48},{80,0},{96,16},{112,32},{1... | collective-permute-start | bytes 4616 | tf_op jit(solution)/shard_map/ppermute | solution.py:291
  178.7 1.5 collective-permute-done.25.refs_7_
  180.2 3.5 %collective-permute-done.27.refs_9_ = f32[1,384]{1,0:T(1,128)S(1)} collective-permute-done((f32[1,384]{1,0:T(1,128)}, f32[1,384]{1,0:T(1,128)S(1)}, u32[]{:S(2)}, u32[]{:S(2)}) %collective-permute-start.27) | collective-permute-done | bytes 1568 | tf_op jit(solution)/shard_map/ppermute | solution.py:291
  183.7 1.7 copy-done.1
  185.4 2.8 %last.1 = (f32[1,384]{1,0:T(1,128)S(1)}, f32[128,2]{1,0:T(8,128)}) custom-call(s32[64]{0:T(128)S(1)} %copy-done.8, bf16[144,2560]{1,0:T(8,128)(2,1)S(1)} %collective-permute-done.7.refs_1_, bf16[112,2560]{1,0:T(8,128)(2,1)S(1)} %collective-permute-done.10.refs_2_, bf16[128,2560]{1,0:T(8,128)(2,1)S(1)} %collective-permute-done.13.refs_3_, ...), custom_call_target="tpu_custom_call" | custom-call | flops 1006632960 | bytes 4587520 | tf_op jit(solution)/shard_map/last/pallas_call | solution.py:242
  188.3 7.8 %all-to-all-start = ((f32[128,1,2]{2,1,0:T(1,128)}), f32[128,1,2]{2,1,0:T(1,128)S(1)}, u32[]{:S(2)}, u32[]{:S(2)}) async-start(f32[128,1,2]{2,1,0:T(1,128)} %bitcast.10), calls=%async_computation | async-start | bytes 131072 | tf_op jit(solution)/shard_map/all_to_all | solution.py:398
  196.1 3.8 %collective-permute-start.34 = (f32[384]{0:T(512)S(1)}, f32[384]{0:T(512)S(1)}, u32[]{:S(2)}, u32[]{:S(2)}) collective-permute-start(f32[384]{0:T(512)S(1)} %reduce.1), channel_id=1, source_target_pairs={{0,96},{16,112},{32,64},{48,80},{64,32},{80,48},{96,0},{112,16},{1... | collective-permute-start | bytes 4616 | tf_op jit(solution)/shard_map/ppermute | solution.py:291
  199.9 5.6 %all-to-all-done = f32[128,1,2]{2,1,0:T(1,128)S(1)} async-done(((f32[128,1,2]{2,1,0:T(1,128)}), f32[128,1,2]{2,1,0:T(1,128)S(1)}, u32[]{:S(2)}, u32[]{:S(2)}) %all-to-all-start) | async-done | bytes 1056 | tf_op jit(solution)/shard_map/all_to_all | solution.py:398
  205.5 0.2 reduce_sum.89
  205.6 0.6 fusion.9
  207.6 0.6 copy.41
  (104 shorter events, 1.4 us)
Async XLA Ops:
  0.6 1.5 copy-start
  2.2 22.5 %copy-start.17 = (s32[1,28]{1,0:T(1,128)S(1)}, s32[1,28]{1,0:T(1,128)}, u32[]{:S(2)}) copy-start(s32[1,28]{1,0:T(1,128)} %param.10) | copy-start | bytes 340
  2.2 23.1 %copy-start.18 = (s32[16]{0:T(128)S(1)}, s32[16]{0:T(128)}, u32[]{:S(2)}) copy-start(s32[16]{0:T(128)} %counts.1) | copy-start | bytes 196
  2.2 57.8 %copy-start.19 = (f32[384]{0:T(512)S(1)}, f32[384]{0:T(512)}, u32[]{:S(2)}) copy-start(f32[384]{0:T(512)} %param.11) | copy-start | bytes 4612
  2.6 0.9 copy-start.4
  3.5 1.6 copy-start.6
  4.8 55.4 %copy-start.5 = (bf16[144,2560]{1,0:T(8,128)(2,1)S(1)}, bf16[144,2560]{1,0:T(8,128)(2,1)}, u32[]{:S(2)}) copy-start(bf16[144,2560]{1,0:T(8,128)(2,1)} %copy-done.4) | copy-start | bytes 2211844
  5.1 0.8 copy-start.2
  7.2 14.0 %copy-start.7 = (bf16[112,2560]{1,0:T(8,128)(2,1)S(1)}, bf16[112,2560]{1,0:T(8,128)(2,1)}, u32[]{:S(2)}) copy-start(bf16[112,2560]{1,0:T(8,128)(2,1)} %copy-done.6) | copy-start | bytes 1720324
  7.2 50.8 %copy-start.3 = (bf16[128,2560]{1,0:T(8,128)(2,1)S(1)}, bf16[128,2560]{1,0:T(8,128)(2,1)}, u32[]{:S(2)}) copy-start(bf16[128,2560]{1,0:T(8,128)(2,1)} %copy-done.2) | copy-start | bytes 1966084
  21.1 119.2 %collective-permute-start.17 = (bf16[16,128,2560]{2,1,0:T(8,128)(2,1)}, bf16[16,128,2560]{2,1,0:T(8,128)(2,1)}, u32[]{:S(2)}, u32[]{:S(2)}) collective-permute-start(bf16[16,128,2560]{2,1,0:T(8,128)(2,1)} %bitcast.17), channel_id=1, source_target_pairs={{0,8},{8,0},{1,9},{9,1},{2,10},{10,2},{3,11},{11,3},{4,12},{12,4},... | collective-permute-start | bytes 31457288 | tf_op jit(solution)/shard_map/ppermute | solution.py:298
  21.1 39.1 %collective-permute-start.15 = (bf16[112,2560]{1,0:T(8,128)(2,1)S(1)}, bf16[112,2560]{1,0:T(8,128)(2,1)}, u32[]{:S(2)}, u32[]{:S(2)}) collective-permute-start(bf16[112,2560]{1,0:T(8,128)(2,1)S(1)} %copy-done.7), channel_id=1, source_target_pairs={{0,16},{16,32},{32,48},{48,0},{64,80},{80,96},{96,112},{112,64},{1... | collective-permute-start | bytes 1720328 | tf_op jit(solution)/shard_map/ppermute | solution.py:291
  23.2 37.1 %collective-permute-start.8 = (bf16[112,2560]{1,0:T(8,128)(2,1)S(1)}, bf16[112,2560]{1,0:T(8,128)(2,1)}, u32[]{:S(2)}, u32[]{:S(2)}) collective-permute-start(bf16[112,2560]{1,0:T(8,128)(2,1)S(1)} %copy-done.7), channel_id=1, source_target_pairs={{0,64},{16,80},{32,96},{48,112},{64,0},{80,16},{96,32},{112,48},{1... | collective-permute-start | bytes 1720328 | tf_op jit(solution)/shard_map/ppermute | solution.py:291
  24.7 13.6 %collective-permute-start = (s32[1,28]{1,0:T(1,128)S(1)}, s32[1,28]{1,0:T(1,128)S(1)}, u32[]{:S(2)}, u32[]{:S(2)}) collective-permute-start(s32[1,28]{1,0:T(1,128)S(1)} %copy-done.17), channel_id=1, source_target_pairs={{0,64},{16,80},{32,96},{48,112},{64,0},{80,16},{96,32},{112,48},{1... | collective-permute-start | bytes 344 | tf_op jit(solution)/shard_map/ppermute | solution.py:291
  25.3 15.5 %collective-permute-start.3 = (s32[16]{0:T(128)S(1)}, s32[16]{0:T(128)S(1)}, u32[]{:S(2)}, u32[]{:S(2)}) collective-permute-start(s32[16]{0:T(128)S(1)} %copy-done.18), channel_id=1, source_target_pairs={{0,8},{8,0},{1,9},{9,1},{2,10},{10,2},{3,11},{11,3},{4,12},{12,4},... | collective-permute-start | bytes 200 | tf_op jit(solution)/shard_map/ppermute | solution.py:298
  38.4 23.5 %collective-permute-start.21 = (bf16[112,2560]{1,0:T(8,128)(2,1)S(1)}, bf16[112,2560]{1,0:T(8,128)(2,1)S(1)}, u32[]{:S(2)}, u32[]{:S(2)}) collective-permute-start(bf16[112,2560]{1,0:T(8,128)(2,1)S(1)} %copy-done.7), channel_id=1, source_target_pairs={{0,48},{16,0},{32,16},{48,32},{64,112},{80,64},{96,80},{112,96},{1... | collective-permute-start | bytes 1720328 | tf_op jit(solution)/shard_map/ppermute | solution.py:291
  40.8 4.9 %collective-permute-start.1 = (s32[2,28]{1,0:T(2,128)S(1)}, s32[2,28]{1,0:T(2,128)S(1)}, u32[]{:S(2)}, u32[]{:S(2)}) collective-permute-start(s32[2,28]{1,0:T(2,128)S(1)} %pad_add_fusion.2), channel_id=1, source_target_pairs={{0,16},{16,32},{32,48},{48,0},{64,80},{80,96},{96,112},{112,64},{1... | collective-permute-start | bytes 680 | tf_op jit(solution)/shard_map/ppermute | solution.py:291
  45.6 7.1 %collective-permute-start.2 = (s32[2,28]{1,0:T(2,128)S(1)}, s32[2,28]{1,0:T(2,128)S(1)}, u32[]{:S(2)}, u32[]{:S(2)}) collective-permute-start(s32[2,28]{1,0:T(2,128)S(1)} %pad_add_fusion.2), channel_id=1, source_target_pairs={{0,48},{16,0},{32,16},{48,32},{64,112},{80,64},{96,80},{112,96},{1... | collective-permute-start | bytes 680 | tf_op jit(solution)/shard_map/ppermute | solution.py:291
  52.8 5.2 %collective-permute-start.4 = (s32[2,28]{1,0:T(2,128)S(1)}, s32[2,28]{1,0:T(2,128)S(1)}, u32[]{:S(2)}, u32[]{:S(2)}) collective-permute-start(s32[2,28]{1,0:T(2,128)S(1)} %collective-permute-done.1), channel_id=1, source_target_pairs={{0,16},{16,32},{32,48},{48,0},{64,80},{80,96},{96,112},{112,64},{1... | collective-permute-start | bytes 680 | tf_op jit(solution)/shard_map/ppermute | solution.py:291
  58.0 14.5 %collective-permute-start.22 = (bf16[128,2560]{1,0:T(8,128)(2,1)S(1)}, bf16[128,2560]{1,0:T(8,128)(2,1)}, u32[]{:S(2)}, u32[]{:S(2)}) collective-permute-start(bf16[128,2560]{1,0:T(8,128)(2,1)S(1)} %copy-done.3), channel_id=1, source_target_pairs={{0,48},{16,0},{32,16},{48,32},{64,112},{80,64},{96,80},{112,96},{1... | collective-permute-start | bytes 1966088 | tf_op jit(solution)/shard_map/ppermute | solution.py:291
  60.2 31.0 %collective-permute-start.5 = (bf16[144,2560]{1,0:T(8,128)(2,1)S(1)}, bf16[144,2560]{1,0:T(8,128)(2,1)S(1)}, u32[]{:S(2)}, u32[]{:S(2)}) collective-permute-start(bf16[144,2560]{1,0:T(8,128)(2,1)S(1)} %copy-done.5), channel_id=1, source_target_pairs={{0,16},{16,32},{32,48},{48,0},{64,80},{80,96},{96,112},{112,64},{1... | collective-permute-start | bytes 2211848 | tf_op jit(solution)/shard_map/ppermute | solution.py:291
  60.3 16.3 %collective-permute-start.11 = (bf16[128,2560]{1,0:T(8,128)(2,1)S(1)}, bf16[128,2560]{1,0:T(8,128)(2,1)}, u32[]{:S(2)}, u32[]{:S(2)}) collective-permute-start(bf16[128,2560]{1,0:T(8,128)(2,1)S(1)} %copy-done.3), channel_id=1, source_target_pairs={{0,64},{16,80},{32,96},{48,112},{64,0},{80,16},{96,32},{112,48},{1... | collective-permute-start | bytes 1966088 | tf_op jit(solution)/shard_map/ppermute | solution.py:291
  61.9 0.8 copy-start.15
  61.9 29.3 %collective-permute-start.19 = (bf16[128,2560]{1,0:T(8,128)(2,1)S(1)}, bf16[128,2560]{1,0:T(8,128)(2,1)}, u32[]{:S(2)}, u32[]{:S(2)}) collective-permute-start(bf16[128,2560]{1,0:T(8,128)(2,1)S(1)} %copy-done.3), channel_id=1, source_target_pairs={{0,16},{16,32},{32,48},{48,0},{64,80},{80,96},{96,112},{112,64},{1... | collective-permute-start | bytes 1966088 | tf_op jit(solution)/shard_map/ppermute | solution.py:291
  72.4 22.5 %collective-permute-start.18 = (bf16[144,2560]{1,0:T(8,128)(2,1)S(1)}, bf16[144,2560]{1,0:T(8,128)(2,1)S(1)}, u32[]{:S(2)}, u32[]{:S(2)}) collective-permute-start(bf16[144,2560]{1,0:T(8,128)(2,1)S(1)} %copy-done.5), channel_id=1, source_target_pairs={{0,64},{16,80},{32,96},{48,112},{64,0},{80,16},{96,32},{112,48},{1... | collective-permute-start | bytes 2211848 | tf_op jit(solution)/shard_map/ppermute | solution.py:291
  76.6 18.8 %collective-permute-start.20 = (bf16[144,2560]{1,0:T(8,128)(2,1)S(1)}, bf16[144,2560]{1,0:T(8,128)(2,1)}, u32[]{:S(2)}, u32[]{:S(2)}) collective-permute-start(bf16[144,2560]{1,0:T(8,128)(2,1)S(1)} %copy-done.5), channel_id=1, source_target_pairs={{0,48},{16,0},{32,16},{48,32},{64,112},{80,64},{96,80},{112,96},{1... | collective-permute-start | bytes 2211848 | tf_op jit(solution)/shard_map/ppermute | solution.py:291
  91.2 13.4 %collective-permute-start.28 = (bf16[112,2560]{1,0:T(8,128)(2,1)}, bf16[112,2560]{1,0:T(8,128)(2,1)S(1)}, u32[]{:S(2)}, u32[]{:S(2)}) collective-permute-start(bf16[112,2560]{1,0:T(8,128)(2,1)} %collective-permute-done.15.refs_8_), channel_id=1, source_target_pairs={{0,16},{16,32},{32,48},{48,0},{64,80},{80,96},{96,112},{112,64},{1... | collective-permute-start | bytes 1720328 | tf_op jit(solution)/shard_map/ppermute | solution.py:291
  91.2 50.0 %copy-start.10 = (bf16[144,2560]{1,0:T(8,128)(2,1)}, bf16[144,2560]{1,0:T(8,128)(2,1)S(1)}, u32[]{:S(2)}) copy-start(bf16[144,2560]{1,0:T(8,128)(2,1)S(1)} %collective-permute-done.5.refs_7_) | copy-start | bytes 2211844
  91.2 16.9 %collective-permute-start.9 = (bf16[112,2560]{1,0:T(8,128)(2,1)}, bf16[112,2560]{1,0:T(8,128)(2,1)}, u32[]{:S(2)}, u32[]{:S(2)}) collective-permute-start(bf16[112,2560]{1,0:T(8,128)(2,1)} %collective-permute-done.8.refs_5_), channel_id=1, source_target_pairs={{0,48},{16,0},{32,16},{48,32},{64,112},{80,64},{96,80},{112,96},{1... | collective-permute-start | bytes 1720328 | tf_op jit(solution)/shard_map/ppermute | solution.py:291
  95.0 46.2 %copy-start.11 = (bf16[144,2560]{1,0:T(8,128)(2,1)}, bf16[144,2560]{1,0:T(8,128)(2,1)S(1)}, u32[]{:S(2)}) copy-start(bf16[144,2560]{1,0:T(8,128)(2,1)S(1)} %collective-permute-done.18.refs_4_) | copy-start | bytes 2211844
  95.0 27.2 %collective-permute-start.29 = (bf16[128,2560]{1,0:T(8,128)(2,1)}, bf16[128,2560]{1,0:T(8,128)(2,1)}, u32[]{:S(2)}, u32[]{:S(2)}) collective-permute-start(bf16[128,2560]{1,0:T(8,128)(2,1)} %collective-permute-done.22.refs_12_), channel_id=1, source_target_pairs={{0,48},{16,0},{32,16},{48,32},{64,112},{80,64},{96,80},{112,96},{1... | collective-permute-start | bytes 1966088 | tf_op jit(solution)/shard_map/ppermute | solution.py:291
  95.2 46.0 %copy-start.20 = (s32[48]{0:T(128)}, s32[48]{0:T(128)S(1)}, u32[]{:S(2)}) copy-start(s32[48]{0:T(128)S(1)} %reshape.94.refs_0_) | copy-start | bytes 580
  95.4 27.7 %collective-permute-start.31 = (bf16[128,2560]{1,0:T(8,128)(2,1)}, bf16[128,2560]{1,0:T(8,128)(2,1)}, u32[]{:S(2)}, u32[]{:S(2)}) collective-permute-start(bf16[128,2560]{1,0:T(8,128)(2,1)} %collective-permute-done.22.refs_12_), channel_id=1, source_target_pairs={{0,64},{16,80},{32,96},{48,112},{64,0},{80,16},{96,32},{112,48},{1... | collective-permute-start | bytes 1966088 | tf_op jit(solution)/shard_map/ppermute | solution.py:291
  104.6 0.8 copy-start.16
  104.6 33.5 %collective-permute-start.6 = (bf16[144,2560]{1,0:T(8,128)(2,1)S(1)}, bf16[144,2560]{1,0:T(8,128)(2,1)S(1)}, u32[]{:S(2)}, u32[]{:S(2)}) collective-permute-start(bf16[144,2560]{1,0:T(8,128)(2,1)S(1)} %collective-permute-done.5.refs_7_), channel_id=1, source_target_pairs={{0,16},{16,32},{32,48},{48,0},{64,80},{80,96},{96,112},{112,64},{1... | collective-permute-start | bytes 2211848 | tf_op jit(solution)/shard_map/ppermute | solution.py:291
  108.1 32.2 %collective-permute-start.30 = (bf16[144,2560]{1,0:T(8,128)(2,1)S(1)}, bf16[144,2560]{1,0:T(8,128)(2,1)S(1)}, u32[]{:S(2)}, u32[]{:S(2)}) collective-permute-start(bf16[144,2560]{1,0:T(8,128)(2,1)S(1)} %collective-permute-done.18.refs_4_), channel_id=1, source_target_pairs={{0,48},{16,0},{32,16},{48,32},{64,112},{80,64},{96,80},{112,96},{1... | collective-permute-start | bytes 2211848 | tf_op jit(solution)/shard_map/ppermute | solution.py:291
  122.2 14.4 %collective-permute-start.12 = (bf16[128,2560]{1,0:T(8,128)(2,1)}, bf16[128,2560]{1,0:T(8,128)(2,1)}, u32[]{:S(2)}, u32[]{:S(2)}) collective-permute-start(bf16[128,2560]{1,0:T(8,128)(2,1)} %collective-permute-done.11.refs_6_), channel_id=1, source_target_pairs={{0,16},{16,32},{32,48},{48,0},{64,80},{80,96},{96,112},{112,64},{1... | collective-permute-start | bytes 1966088 | tf_op jit(solution)/shard_map/ppermute | solution.py:291
  123.2 37.8 %collective-permute-start.14 = (bf16[144,2560]{1,0:T(8,128)(2,1)S(1)}, bf16[144,2560]{1,0:T(8,128)(2,1)S(1)}, u32[]{:S(2)}, u32[]{:S(2)}) collective-permute-start(bf16[144,2560]{1,0:T(8,128)(2,1)S(1)} %collective-permute-done.5.refs_7_), channel_id=1, source_target_pairs={{0,64},{16,80},{32,96},{48,112},{64,0},{80,16},{96,32},{112,48},{1... | collective-permute-start | bytes 2211848 | tf_op jit(solution)/shard_map/ppermute | solution.py:291
  125.3 25.4 %copy-start.21 = (f32[1,384]{1,0:T(1,128)S(1)}, f32[1,384]{1,0:T(1,128)}, u32[]{:S(2)}) copy-start(f32[1,384]{1,0:T(1,128)} %get-tuple-element.21) | copy-start | bytes 4612
  125.3 26.1 %copy-start.22 = (f32[1,384]{1,0:T(1,128)S(1)}, f32[1,384]{1,0:T(1,128)}, u32[]{:S(2)}) copy-start(f32[1,384]{1,0:T(1,128)} %get-tuple-element.23) | copy-start | bytes 4612
  136.6 21.6 %collective-permute-start.16 = (bf16[112,2560]{1,0:T(8,128)(2,1)}, bf16[112,2560]{1,0:T(8,128)(2,1)S(1)}, u32[]{:S(2)}, u32[]{:S(2)}) collective-permute-start(bf16[112,2560]{1,0:T(8,128)(2,1)} %collective-permute-done.15.refs_8_), channel_id=1, source_target_pairs={{0,64},{16,80},{32,96},{48,112},{64,0},{80,16},{96,32},{112,48},{1... | collective-permute-start | bytes 1720328 | tf_op jit(solution)/shard_map/ppermute | solution.py:291
  138.0 12.6 %copy-start.12 = (bf16[144,2560]{1,0:T(8,128)(2,1)}, bf16[144,2560]{1,0:T(8,128)(2,1)S(1)}, u32[]{:S(2)}) copy-start(bf16[144,2560]{1,0:T(8,128)(2,1)S(1)} %collective-permute-done.6.refs_1_) | copy-start | bytes 2211844
  138.0 27.2 %collective-permute-start.10 = (bf16[112,2560]{1,0:T(8,128)(2,1)}, bf16[112,2560]{1,0:T(8,128)(2,1)S(1)}, u32[]{:S(2)}, u32[]{:S(2)}) collective-permute-start(bf16[112,2560]{1,0:T(8,128)(2,1)} %collective-permute-done.9.refs_5_), channel_id=1, source_target_pairs={{0,48},{16,0},{32,16},{48,32},{64,112},{80,64},{96,80},{112,96},{1... | collective-permute-start | bytes 1720328 | tf_op jit(solution)/shard_map/ppermute | solution.py:291
  140.4 10.3 %copy-start.13 = (bf16[144,2560]{1,0:T(8,128)(2,1)}, bf16[144,2560]{1,0:T(8,128)(2,1)S(1)}, u32[]{:S(2)}) copy-start(bf16[144,2560]{1,0:T(8,128)(2,1)S(1)} %collective-permute-done.30.refs_4_) | copy-start | bytes 2211844
  140.4 31.1 %collective-permute-start.13 = (bf16[128,2560]{1,0:T(8,128)(2,1)}, bf16[128,2560]{1,0:T(8,128)(2,1)S(1)}, u32[]{:S(2)}, u32[]{:S(2)}) collective-permute-start(bf16[128,2560]{1,0:T(8,128)(2,1)} %collective-permute-done.12.refs_3_), channel_id=1, source_target_pairs={{0,16},{16,32},{32,48},{48,0},{64,80},{80,96},{96,112},{112,64},{1... | collective-permute-start | bytes 1966088 | tf_op jit(solution)/shard_map/ppermute | solution.py:291
  140.4 34.1 %collective-permute-start.7 = (bf16[144,2560]{1,0:T(8,128)(2,1)S(1)}, bf16[144,2560]{1,0:T(8,128)(2,1)S(1)}, u32[]{:S(2)}, u32[]{:S(2)}) collective-permute-start(bf16[144,2560]{1,0:T(8,128)(2,1)S(1)} %collective-permute-done.6.refs_1_), channel_id=1, source_target_pairs={{0,64},{16,80},{32,96},{48,112},{64,0},{80,16},{96,32},{112,48},{1... | collective-permute-start | bytes 2211848 | tf_op jit(solution)/shard_map/ppermute | solution.py:291
  158.2 7.1 %copy-start.14 = (bf16[112,2560]{1,0:T(8,128)(2,1)}, bf16[112,2560]{1,0:T(8,128)(2,1)S(1)}, u32[]{:S(2)}) copy-start(bf16[112,2560]{1,0:T(8,128)(2,1)S(1)} %collective-permute-done.16.refs_2_) | copy-start | bytes 1720324
  158.2 16.3 %collective-permute-start.32 = (f32[1,384]{1,0:T(1,128)}, f32[1,384]{1,0:T(1,128)S(1)}, u32[]{:S(2)}, u32[]{:S(2)}) collective-permute-start(f32[1,384]{1,0:T(1,128)} %get-tuple-element.28), channel_id=1, source_target_pairs={{0,64},{16,80},{32,96},{48,112},{64,0},{80,16},{96,32},{112,48},{1... | collective-permute-start | bytes 4616 | tf_op jit(solution)/shard_map/ppermute | solution.py:291
  161.0 4.3 %copy-start.9 = (bf16[144,2560]{1,0:T(8,128)(2,1)}, bf16[144,2560]{1,0:T(8,128)(2,1)S(1)}, u32[]{:S(2)}) copy-start(bf16[144,2560]{1,0:T(8,128)(2,1)S(1)} %collective-permute-done.14.refs_1_) | copy-start | bytes 2211844
  161.0 10.5 %copy-start.25 = (f32[1,384]{1,0:T(1,128)S(1)}, f32[1,384]{1,0:T(1,128)}, u32[]{:S(2)}) copy-start(f32[1,384]{1,0:T(1,128)} %get-tuple-element.24) | copy-start | bytes 4612
  161.0 13.5 %copy-start.24 = (f32[1,384]{1,0:T(1,128)S(1)}, f32[1,384]{1,0:T(1,128)}, u32[]{:S(2)}) copy-start(f32[1,384]{1,0:T(1,128)} %get-tuple-element.25) | copy-start | bytes 4612
  161.0 13.6 %copy-start.23 = (f32[1,384]{1,0:T(1,128)S(1)}, f32[1,384]{1,0:T(1,128)}, u32[]{:S(2)}) copy-start(f32[1,384]{1,0:T(1,128)} %get-tuple-element.26) | copy-start | bytes 4612
  161.0 22.7 %copy-start.8 = (s32[64]{0:T(128)S(1)}, s32[64]{0:T(128)}, u32[]{:S(2)}) copy-start(s32[64]{0:T(128)} %pad_add_fusion.8.refs_0_) | copy-start | bytes 772
  161.0 17.7 %collective-permute-start.33 = (f32[1,384]{1,0:T(1,128)}, f32[1,384]{1,0:T(1,128)S(1)}, u32[]{:S(2)}, u32[]{:S(2)}) collective-permute-start(f32[1,384]{1,0:T(1,128)} %get-tuple-element.29), channel_id=1, source_target_pairs={{0,48},{16,0},{32,16},{48,32},{64,112},{80,64},{96,80},{112,96},{1... | collective-permute-start | bytes 4616 | tf_op jit(solution)/shard_map/ppermute | solution.py:291
  165.3 18.4 %collective-permute-start.23 = (f32[3,384]{1,0:T(4,128)S(1)}, f32[3,384]{1,0:T(4,128)S(1)}, u32[]{:S(2)}, u32[]{:S(2)}) collective-permute-start(f32[3,384]{1,0:T(4,128)S(1)} %pad_maximum_fusion), channel_id=1, source_target_pairs={{0,96},{16,112},{32,64},{48,80},{64,32},{80,48},{96,0},{112,16},{1... | collective-permute-start | bytes 13832 | tf_op jit(solution)/shard_map/ppermute | solution.py:291
  171.4 7.2 %collective-permute-start.24 = (f32[1,384]{1,0:T(1,128)S(1)}, f32[1,384]{1,0:T(1,128)S(1)}, u32[]{:S(2)}, u32[]{:S(2)}) collective-permute-start(f32[1,384]{1,0:T(1,128)S(1)} %copy-done.25), channel_id=1, source_target_pairs={{0,32},{16,48},{32,0},{48,16},{64,96},{80,112},{96,64},{112,80},{1... | collective-permute-start | bytes 4616 | tf_op jit(solution)/shard_map/ppermute | solution.py:291
  174.5 5.7 %collective-permute-start.25 = (f32[1,384]{1,0:T(1,128)S(1)}, f32[1,384]{1,0:T(1,128)S(1)}, u32[]{:S(2)}, u32[]{:S(2)}) collective-permute-start(f32[1,384]{1,0:T(1,128)S(1)} %copy-done.24), channel_id=1, source_target_pairs={{0,80},{16,96},{32,112},{48,64},{64,16},{80,32},{96,48},{112,0},{1... | collective-permute-start | bytes 4616 | tf_op jit(solution)/shard_map/ppermute | solution.py:291
  174.5 5.7 %collective-permute-start.26 = (f32[1,384]{1,0:T(1,128)S(1)}, f32[1,384]{1,0:T(1,128)S(1)}, u32[]{:S(2)}, u32[]{:S(2)}) collective-permute-start(f32[1,384]{1,0:T(1,128)S(1)} %copy-done.23), channel_id=1, source_target_pairs={{0,112},{16,64},{32,80},{48,96},{64,48},{80,0},{96,16},{112,32},{1... | collective-permute-start | bytes 4616 | tf_op jit(solution)/shard_map/ppermute | solution.py:291
  178.7 5.0 %collective-permute-start.27 = (f32[1,384]{1,0:T(1,128)}, f32[1,384]{1,0:T(1,128)S(1)}, u32[]{:S(2)}, u32[]{:S(2)}) collective-permute-start(f32[1,384]{1,0:T(1,128)} %get-tuple-element.27), channel_id=1, source_target_pairs={{0,16},{16,32},{32,48},{48,0},{64,80},{80,96},{96,112},{112,64},{1... | collective-permute-start | bytes 4616 | tf_op jit(solution)/shard_map/ppermute | solution.py:291
  183.7 1.7 copy-start.1
  188.3 17.2 %all-to-all-start = ((f32[128,1,2]{2,1,0:T(1,128)}), f32[128,1,2]{2,1,0:T(1,128)S(1)}, u32[]{:S(2)}, u32[]{:S(2)}) async-start(f32[128,1,2]{2,1,0:T(1,128)} %bitcast.10), calls=%async_computation | async-start | bytes 131072 | tf_op jit(solution)/shard_map/all_to_all | solution.py:398
  196.1 11.5 %collective-permute-start.34 = (f32[384]{0:T(512)S(1)}, f32[384]{0:T(512)S(1)}, u32[]{:S(2)}, u32[]{:S(2)}) collective-permute-start(f32[384]{0:T(512)S(1)} %reduce.1), channel_id=1, source_target_pairs={{0,96},{16,112},{32,64},{48,80},{64,32},{80,48},{96,0},{112,16},{1... | collective-permute-start | bytes 4616 | tf_op jit(solution)/shard_map/ppermute | solution.py:291

commit v3 on v2

--- a/solution.py
+++ b/solution.py
@@ -263,6 +263,20 @@
     )(table, *pieces, keys, base, *parts)
 
 
+def mean_kernel(shares, mean):
+    sums = jnp.sum(shares[...], axis=0, keepdims=True)
+    mean[...] = sums[:, 0:1] / sums[:, 1:2]
+
+
+def mean_of(shares):
+    return pl.pallas_call(
+        mean_kernel,
+        out_shape=jax.ShapeDtypeStruct((1, 1), jnp.float32),
+        compiler_params=pltpu.CompilerParams(vmem_limit_bytes=4 * 2**20),
+        name="ratio",
+    )(shares)
+
+
 def slot_table(lists, device, blocks_here, counts):
     owner = lists // blocks_here
     block = lists % blocks_here
@@ -396,8 +410,8 @@
     )
     query_loss = shift(query_loss[0], 1, half)
     shares = lax.all_to_all(shares, GRP_REP, split_axis=0, concat_axis=0, tiled=True)
-    sums = jnp.sum(shares, axis=0)
-    return (query_loss, sums[0] / sums[1])
+    mean = mean_of(shares)
+    return (query_loss, mean[0, 0])
 
 
 def solution(mesh):

time: 210 us -> 210 us (level)
  blocking collectives: 0 us -> 20.4 us
  starting transfers between devices: 57.7 us -> 46.2 us
  waiting for transfers between devices: 94.3 us -> 88.8 us
  between operations: 3.49 us -> 1.01 us
    all_to_all x0 -> x1, blocking collectives: none -> 20.4 us  [local(): lax.all_to_all(shares, GRP_REP, split_axis=0, concat_axis=0, tiled=True)]
    all_to_all x1 -> x0, starting transfers between devices: 7.77 us -> none  [local(): lax.all_to_all(shares, GRP_REP, split_axis=0, concat_axis=0, tiled=True)]
    all_to_all x1 -> x0, waiting for transfers between devices: 5.56 us -> none  [local(): lax.all_to_all(shares, GRP_REP, split_axis=0, concat_axis=0, tiled=True)]
    ppermute x33, starting transfers between devices: 49.9 us -> 46.2 us  [shift(): return lax.ppermute(a, PLANE, pairs)]
  transfers between devices with their start and end apart: 36 -> 35, of which waited for: 14 -> 13; matrix products, arithmetic and copies ran while one was open for 2% -> 2% of each run, Pallas kernels for 11% -> 11%
where the time goes in v3:
time: 210 us; the launch traced here: 209 us
  waiting for transfers between devices  88.8 us (42%)
  starting transfers between devices  46.2 us (22%)
  Pallas kernels  39.8 us (19%)
  blocking collectives  20.4 us (10%)
  local copies, waits for them, and re-layouts  10.4 us (5%)
  other arithmetic  2.85 us (1%)
    ppermute x33, waiting for transfers between devices, shift(): return lax.ppermute(a, PLANE, pairs)  88.8 us
    ppermute x33, starting transfers between devices, shift(): return lax.ppermute(a, PLANE, pairs)  46.2 us
    pallas_call x3, Pallas kernels, score_listed(): pl.pallas_call(kernel, in_specs=[pl.BlockSpec(memory_space=pltpu.SMEM)] +...  22.4 us
    all_to_all x1, blocking collectives, local(): lax.all_to_all(shares, GRP_REP, split_axis=0, concat_axis=0, tiled=True)  20.4 us
    pallas_call x1, Pallas kernels, score_local(): pl.pallas_call(local_kernel, grid_spec=pltpu.PrefetchScalarGridSpec(num_s...  13.9 us
    unnamed x53, local copies, waits for them, and re-layouts  7.06 us
  transfers between devices with their start and end apart: 35, of which 13 were waited for; matrix products, arithmetic and copies ran while one was open for 2% of the time, Pallas kernels for 11%

profile of v3, /device:TPU:0, one launch (start us, length us, event | category | flops | bytes accessed | tf_op | source)
XLA Modules:
  0.0 209.4 jit_solution(12579835962680280211)
XLA Ops:
  0.6 1.5 copy-done
  2.2 0.4 shard_map.77
  2.6 0.9 copy-done.4
  3.5 1.3 slice.3.queries
  4.8 0.2 shard_map.78.c.refs_3_
  5.1 0.8 copy-done.2
  5.9 1.2 broadcast_in_dim.82.positive
  7.2 13.9 %local.1 = (bf16[2048,2560]{1,0:T(8,128)(2,1)}, f32[1,384]{1,0:T(1,128)}, f32[1,384]{1,0:T(1,128)}) custom-call(s32[16]{0:T(128)} %counts.1, bf16[144,2560]{1,0:T(8,128)(2,1)} %copy-done.4, bf16[112,2560]{1,0:T(8,128)(2,1)} %copy-done.6, bf16[128,2560]{1,0:T(8,128)(2,1)} %copy-done.2, s32[1,384]{1,0:T(1,128)} %broadcast_in_dim.82.positive, ...), custom_call_target="tpu_custom_call" | custom-call | flops 4026531840 | bytes 20971520 | tf_op jit(solution)/shard_map/local/pallas_call | solution.py:95
  21.1 2.1 collective-permute-start.15
  23.2 1.5 collective-permute-start.8
  24.7 0.5 collective-permute-start
  25.3 13.1 %collective-permute-done = s32[1,28]{1,0:T(1,128)S(1)} collective-permute-done((s32[1,28]{1,0:T(1,128)S(1)}, s32[1,28]{1,0:T(1,128)S(1)}, u32[]{:S(2)}, u32[]{:S(2)}) %collective-permute-start) | collective-permute-done | bytes 144 | tf_op jit(solution)/shard_map/ppermute | solution.py:305
  38.4 2.4 %collective-permute-start.21 = (bf16[112,2560]{1,0:T(8,128)(2,1)S(1)}, bf16[112,2560]{1,0:T(8,128)(2,1)S(1)}, u32[]{:S(2)}, u32[]{:S(2)}) collective-permute-start(bf16[112,2560]{1,0:T(8,128)(2,1)S(1)} %copy-done.7), channel_id=1, source_target_pairs={{0,48},{16,0},{32,16},{48,32},{64,112},{80,64},{96,80},{112,96},{1... | collective-permute-start | bytes 1720328 | tf_op jit(solution)/shard_map/ppermute | solution.py:305
  40.9 4.8 %collective-permute-done.1 = s32[2,28]{1,0:T(2,128)S(1)} collective-permute-done((s32[2,28]{1,0:T(2,128)S(1)}, s32[2,28]{1,0:T(2,128)S(1)}, u32[]{:S(2)}, u32[]{:S(2)}) %collective-permute-start.1) | collective-permute-done | bytes 256 | tf_op jit(solution)/shard_map/ppermute | solution.py:305
  45.6 0.5 collective-permute-start.2
  46.2 6.6 %collective-permute-done.2 = s32[2,28]{1,0:T(2,128)S(1)} collective-permute-done((s32[2,28]{1,0:T(2,128)S(1)}, s32[2,28]{1,0:T(2,128)S(1)}, u32[]{:S(2)}, u32[]{:S(2)}) %collective-permute-start.2) | collective-permute-done | bytes 256 | tf_op jit(solution)/shard_map/ppermute | solution.py:305
  52.8 1.7 collective-permute-start.4
  54.5 3.4 %collective-permute-done.4 = s32[2,28]{1,0:T(2,128)S(1)} collective-permute-done((s32[2,28]{1,0:T(2,128)S(1)}, s32[2,28]{1,0:T(2,128)S(1)}, u32[]{:S(2)}, u32[]{:S(2)}) %collective-permute-start.4) | collective-permute-done | bytes 256 | tf_op jit(solution)/shard_map/ppermute | solution.py:305
  58.0 2.0 collective-permute-start.22
  60.0 0.2 select_reduce_fusion.3
  60.3 1.6 collective-permute-start.11
  61.9 0.1 collective-permute-start.19
  62.0 0.1 copy.31
  62.1 0.6 copy-done.15
  62.7 9.7 %collective-permute-done.22.refs_12_ = bf16[128,2560]{1,0:T(8,128)(2,1)} collective-permute-done((bf16[128,2560]{1,0:T(8,128)(2,1)S(1)}, bf16[128,2560]{1,0:T(8,128)(2,1)}, u32[]{:S(2)}, u32[]{:S(2)}) %collective-permute-start.22) | collective-permute-done | bytes 655392 | tf_op jit(solution)/shard_map/ppermute | solution.py:305
  72.4 1.5 collective-permute-start.18
  73.9 0.1 copy.32
  74.0 2.6 %collective-permute-done.11.refs_6_ = bf16[128,2560]{1,0:T(8,128)(2,1)} collective-permute-done((bf16[128,2560]{1,0:T(8,128)(2,1)S(1)}, bf16[128,2560]{1,0:T(8,128)(2,1)}, u32[]{:S(2)}, u32[]{:S(2)}) %collective-permute-start.11) | collective-permute-done | bytes 655392 | tf_op jit(solution)/shard_map/ppermute | solution.py:305
  76.6 3.0 %collective-permute-start.20 = (bf16[144,2560]{1,0:T(8,128)(2,1)S(1)}, bf16[144,2560]{1,0:T(8,128)(2,1)}, u32[]{:S(2)}, u32[]{:S(2)}) collective-permute-start(bf16[144,2560]{1,0:T(8,128)(2,1)S(1)} %copy-done.5), channel_id=1, source_target_pairs={{0,48},{16,0},{32,16},{48,32},{64,112},{80,64},{96,80},{112,96},{1... | collective-permute-start | bytes 2211848 | tf_op jit(solution)/shard_map/ppermute | solution.py:305
  79.7 11.5 %collective-permute-done.19.refs_9_ = bf16[128,2560]{1,0:T(8,128)(2,1)} collective-permute-done((bf16[128,2560]{1,0:T(8,128)(2,1)S(1)}, bf16[128,2560]{1,0:T(8,128)(2,1)}, u32[]{:S(2)}, u32[]{:S(2)}) %collective-permute-start.19) | collective-permute-done | bytes 655392 | tf_op jit(solution)/shard_map/ppermute | solution.py:305
  91.2 3.2 %collective-permute-start.9 = (bf16[112,2560]{1,0:T(8,128)(2,1)}, bf16[112,2560]{1,0:T(8,128)(2,1)}, u32[]{:S(2)}, u32[]{:S(2)}) collective-permute-start(bf16[112,2560]{1,0:T(8,128)(2,1)} %collective-permute-done.8.refs_5_), channel_id=1, source_target_pairs={{0,48},{16,0},{32,16},{48,32},{64,112},{80,64},{96,80},{112,96},{1... | collective-permute-start | bytes 1720328 | tf_op jit(solution)/shard_map/ppermute | solution.py:305
  94.5 0.2 fusion
  94.7 0.2 fusion.1
  95.2 0.2 select_reduce_fusion.7
  95.4 1.6 collective-permute-start.31
  97.0 7.6 %collective-permute-done.28.refs_2_ = bf16[112,2560]{1,0:T(8,128)(2,1)S(1)} collective-permute-done((bf16[112,2560]{1,0:T(8,128)(2,1)}, bf16[112,2560]{1,0:T(8,128)(2,1)S(1)}, u32[]{:S(2)}, u32[]{:S(2)}) %collective-permute-start.28) | collective-permute-done | bytes 573472 | tf_op jit(solution)/shard_map/ppermute | solution.py:305
  104.6 0.8 copy-done.16
  105.4 2.8 %collective-permute-done.9.refs_5_ = bf16[112,2560]{1,0:T(8,128)(2,1)} collective-permute-done((bf16[112,2560]{1,0:T(8,128)(2,1)}, bf16[112,2560]{1,0:T(8,128)(2,1)}, u32[]{:S(2)}, u32[]{:S(2)}) %collective-permute-start.9) | collective-permute-done | bytes 573472 | tf_op jit(solution)/shard_map/ppermute | solution.py:305
  108.1 3.7 %collective-permute-start.30 = (bf16[144,2560]{1,0:T(8,128)(2,1)S(1)}, bf16[144,2560]{1,0:T(8,128)(2,1)S(1)}, u32[]{:S(2)}, u32[]{:S(2)}) collective-permute-start(bf16[144,2560]{1,0:T(8,128)(2,1)S(1)} %collective-permute-done.18.refs_4_), channel_id=1, source_target_pairs={{0,48},{16,0},{32,16},{48,32},{64,112},{80,64},{96,80},{112,96},{1... | collective-permute-start | bytes 2211848 | tf_op jit(solution)/shard_map/ppermute | solution.py:305
  111.8 10.3 %collective-permute-done.29.refs_3_ = bf16[128,2560]{1,0:T(8,128)(2,1)} collective-permute-done((bf16[128,2560]{1,0:T(8,128)(2,1)}, bf16[128,2560]{1,0:T(8,128)(2,1)}, u32[]{:S(2)}, u32[]{:S(2)}) %collective-permute-start.29) | collective-permute-done | bytes 655392 | tf_op jit(solution)/shard_map/ppermute | solution.py:305
  122.4 0.1 copy.36
  122.6 0.2 fusion.3
  122.8 0.2 fusion.4
  123.2 1.5 collective-permute-start.14
  124.7 0.6 pad_add_fusion.8.refs_0_
  125.3 11.3 %collective-permute-done.12.refs_3_ = bf16[128,2560]{1,0:T(8,128)(2,1)} collective-permute-done((bf16[128,2560]{1,0:T(8,128)(2,1)}, bf16[128,2560]{1,0:T(8,128)(2,1)}, u32[]{:S(2)}, u32[]{:S(2)}) %collective-permute-start.12) | collective-permute-done | bytes 655392 | tf_op jit(solution)/shard_map/ppermute | solution.py:305
  136.6 1.5 collective-permute-start.16
  138.0 2.3 %collective-permute-start.10 = (bf16[112,2560]{1,0:T(8,128)(2,1)}, bf16[112,2560]{1,0:T(8,128)(2,1)S(1)}, u32[]{:S(2)}, u32[]{:S(2)}) collective-permute-start(bf16[112,2560]{1,0:T(8,128)(2,1)} %collective-permute-done.9.refs_5_), channel_id=1, source_target_pairs={{0,48},{16,0},{32,16},{48,32},{64,112},{80,64},{96,80},{112,96},{1... | collective-permute-start | bytes 1720328 | tf_op jit(solution)/shard_map/ppermute | solution.py:305
  140.4 0.8 collective-permute-start.7
  141.2 9.4 %listed.4 = (f32[1,384]{1,0:T(1,128)}, f32[1,384]{1,0:T(1,128)}, f32[1,384]{1,0:T(1,128)}, f32[1,384]{1,0:T(1,128)}) custom-call(s32[48]{0:T(128)} %copy-done.20, bf16[144,2560]{1,0:T(8,128)(2,1)} %copy-done.4, bf16[112,2560]{1,0:T(8,128)(2,1)} %copy-done.6, bf16[128,2560]{1,0:T(8,128)(2,1)} %copy-done.2, bf16[144,2560]{1,0:T(8,128)(2,1)} %copy-done.11, ...), custom_call_target="tpu_custom_call" | custom-call | flops 4026531840 | bytes 18350080 | tf_op jit(solution)/shard_map/listed/pallas_call | solution.py:187
  150.7 0.7 add.39
  151.4 6.8 %listed.5 = (f32[1,384]{1,0:T(1,128)}, f32[1,384]{1,0:T(1,128)}) custom-call(s32[64]{0:T(128)} %pad_add_fusion.8.refs_0_, bf16[144,2560]{1,0:T(8,128)(2,1)} %copy-done.12, bf16[112,2560]{1,0:T(8,128)(2,1)} %copy-done.16, bf16[128,2560]{1,0:T(8,128)(2,1)} %collective-permute-done.29.refs_3_, bf16[144,2560]{1,0:T(8,128)(2,1)} %copy-done.13, ...), custom_call_target="tpu_custom_call" | custom-call | flops 2013265920 | bytes 9175040 | tf_op jit(solution)/shard_map/listed/pallas_call | solution.py:187
  158.2 2.8 %collective-permute-start.32 = (f32[1,384]{1,0:T(1,128)}, f32[1,384]{1,0:T(1,128)S(1)}, u32[]{:S(2)}, u32[]{:S(2)}) collective-permute-start(f32[1,384]{1,0:T(1,128)} %get-tuple-element.28), channel_id=1, source_target_pairs={{0,64},{16,80},{32,96},{48,112},{64,0},{80,16},{96,32},{112,48},{1... | collective-permute-start | bytes 4616 | tf_op jit(solution)/shard_map/ppermute | solution.py:305
  161.0 4.2 %collective-permute-start.33 = (f32[1,384]{1,0:T(1,128)}, f32[1,384]{1,0:T(1,128)S(1)}, u32[]{:S(2)}, u32[]{:S(2)}) collective-permute-start(f32[1,384]{1,0:T(1,128)} %get-tuple-element.29), channel_id=1, source_target_pairs={{0,48},{16,0},{32,16},{48,32},{64,112},{80,64},{96,80},{112,96},{1... | collective-permute-start | bytes 4616 | tf_op jit(solution)/shard_map/ppermute | solution.py:305
  165.3 6.1 %listed.3 = (f32[1,384]{1,0:T(1,128)}, bf16[512,2560]{1,0:T(8,128)(2,1)}) custom-call(s32[64]{0:T(128)} %pad_add_fusion.8.refs_0_, bf16[144,2560]{1,0:T(8,128)(2,1)} %copy-done.9, bf16[112,2560]{1,0:T(8,128)(2,1)} %copy-done.14, bf16[128,2560]{1,0:T(8,128)(2,1)} %collective-permute-done.12.refs_3_, bf16[16,128,2560]{2,1,0:T(8,128)(2,1)} %bitcast.23, ...), custom_call_target="tpu_custom_call" | custom-call | flops 1006632960 | bytes 7208960 | tf_op jit(solution)/shard_map/listed/pallas_call | solution.py:187
  171.4 3.1 %collective-permute-start.24 = (f32[1,384]{1,0:T(1,128)S(1)}, f32[1,384]{1,0:T(1,128)S(1)}, u32[]{:S(2)}, u32[]{:S(2)}) collective-permute-start(f32[1,384]{1,0:T(1,128)S(1)} %copy-done.25), channel_id=1, source_target_pairs={{0,32},{16,48},{32,0},{48,16},{64,96},{80,112},{96,64},{112,80},{1... | collective-permute-start | bytes 4616 | tf_op jit(solution)/shard_map/ppermute | solution.py:305
  174.5 4.1 %collective-permute-start.26 = (f32[1,384]{1,0:T(1,128)S(1)}, f32[1,384]{1,0:T(1,128)S(1)}, u32[]{:S(2)}, u32[]{:S(2)}) collective-permute-start(f32[1,384]{1,0:T(1,128)S(1)} %copy-done.23), channel_id=1, source_target_pairs={{0,112},{16,64},{32,80},{48,96},{64,48},{80,0},{96,16},{112,32},{1... | collective-permute-start | bytes 4616 | tf_op jit(solution)/shard_map/ppermute | solution.py:305
  178.7 1.5 collective-permute-done.25.refs_7_
  180.2 3.5 %collective-permute-done.27.refs_9_ = f32[1,384]{1,0:T(1,128)S(1)} collective-permute-done((f32[1,384]{1,0:T(1,128)}, f32[1,384]{1,0:T(1,128)S(1)}, u32[]{:S(2)}, u32[]{:S(2)}) %collective-permute-start.27) | collective-permute-done | bytes 1568 | tf_op jit(solution)/shard_map/ppermute | solution.py:305
  183.7 1.7 copy-done.1
  185.4 2.2 %last.1 = (f32[1,384]{1,0:T(1,128)S(1)}, f32[128,2]{1,0:T(8,128)S(1)}) custom-call(s32[64]{0:T(128)S(1)} %copy-done.8, bf16[144,2560]{1,0:T(8,128)(2,1)S(1)} %collective-permute-done.7.refs_1_, bf16[112,2560]{1,0:T(8,128)(2,1)S(1)} %collective-permute-done.10.refs_2_, bf16[128,2560]{1,0:T(8,128)(2,1)S(1)} %collective-permute-done.13.refs_3_, ...), custom_call_target="tpu_custom_call" | custom-call | flops 1006632960 | bytes 4587520 | tf_op jit(solution)/shard_map/last/pallas_call | solution.py:242
  187.8 20.4 %all_to_all.11 = f32[128,1,2]{2,1,0:T(1,128)S(1)} all-to-all(f32[128,1,2]{2,1,0:T(1,128)S(1)} %bitcast.19), channel_id=1, replica_groups=mesh['grp_0'=2,'grp_1'=4,'grp_2'=2,'rep_0'=4,'rep_1'=2] {'grp_0','grp_1'..., dimensions={0} | all-to-all | bytes 2048 | tf_op jit(solution)/shard_map/all_to_all | solution.py:412
  208.2 0.6 ratio.1
  208.8 0.6 copy.41
  (102 shorter events, 1.2 us)
Async XLA Ops:
  0.6 1.5 copy-start
  2.2 22.5 %copy-start.17 = (s32[1,28]{1,0:T(1,128)S(1)}, s32[1,28]{1,0:T(1,128)}, u32[]{:S(2)}) copy-start(s32[1,28]{1,0:T(1,128)} %param.10) | copy-start | bytes 340
  2.2 23.1 %copy-start.18 = (s32[16]{0:T(128)S(1)}, s32[16]{0:T(128)}, u32[]{:S(2)}) copy-start(s32[16]{0:T(128)} %counts.1) | copy-start | bytes 196
  2.2 57.8 %copy-start.19 = (f32[384]{0:T(512)S(1)}, f32[384]{0:T(512)}, u32[]{:S(2)}) copy-start(f32[384]{0:T(512)} %param.11) | copy-start | bytes 4612
  2.6 0.9 copy-start.4
  3.5 1.6 copy-start.6
  4.8 55.4 %copy-start.5 = (bf16[144,2560]{1,0:T(8,128)(2,1)S(1)}, bf16[144,2560]{1,0:T(8,128)(2,1)}, u32[]{:S(2)}) copy-start(bf16[144,2560]{1,0:T(8,128)(2,1)} %copy-done.4) | copy-start | bytes 2211844
  5.1 0.8 copy-start.2
  7.2 14.0 %copy-start.7 = (bf16[112,2560]{1,0:T(8,128)(2,1)S(1)}, bf16[112,2560]{1,0:T(8,128)(2,1)}, u32[]{:S(2)}) copy-start(bf16[112,2560]{1,0:T(8,128)(2,1)} %copy-done.6) | copy-start | bytes 1720324
  7.2 50.8 %copy-start.3 = (bf16[128,2560]{1,0:T(8,128)(2,1)S(1)}, bf16[128,2560]{1,0:T(8,128)(2,1)}, u32[]{:S(2)}) copy-start(bf16[128,2560]{1,0:T(8,128)(2,1)} %copy-done.2) | copy-start | bytes 1966084
  21.1 119.2 %collective-permute-start.17 = (bf16[16,128,2560]{2,1,0:T(8,128)(2,1)}, bf16[16,128,2560]{2,1,0:T(8,128)(2,1)}, u32[]{:S(2)}, u32[]{:S(2)}) collective-permute-start(bf16[16,128,2560]{2,1,0:T(8,128)(2,1)} %bitcast.20), channel_id=1, source_target_pairs={{0,8},{8,0},{1,9},{9,1},{2,10},{10,2},{3,11},{11,3},{4,12},{12,4},... | collective-permute-start | bytes 31457288 | tf_op jit(solution)/shard_map/ppermute | solution.py:312
  21.1 39.1 %collective-permute-start.15 = (bf16[112,2560]{1,0:T(8,128)(2,1)S(1)}, bf16[112,2560]{1,0:T(8,128)(2,1)}, u32[]{:S(2)}, u32[]{:S(2)}) collective-permute-start(bf16[112,2560]{1,0:T(8,128)(2,1)S(1)} %copy-done.7), channel_id=1, source_target_pairs={{0,16},{16,32},{32,48},{48,0},{64,80},{80,96},{96,112},{112,64},{1... | collective-permute-start | bytes 1720328 | tf_op jit(solution)/shard_map/ppermute | solution.py:305
  23.2 37.1 %collective-permute-start.8 = (bf16[112,2560]{1,0:T(8,128)(2,1)S(1)}, bf16[112,2560]{1,0:T(8,128)(2,1)}, u32[]{:S(2)}, u32[]{:S(2)}) collective-permute-start(bf16[112,2560]{1,0:T(8,128)(2,1)S(1)} %copy-done.7), channel_id=1, source_target_pairs={{0,64},{16,80},{32,96},{48,112},{64,0},{80,16},{96,32},{112,48},{1... | collective-permute-start | bytes 1720328 | tf_op jit(solution)/shard_map/ppermute | solution.py:305
  24.7 13.6 %collective-permute-start = (s32[1,28]{1,0:T(1,128)S(1)}, s32[1,28]{1,0:T(1,128)S(1)}, u32[]{:S(2)}, u32[]{:S(2)}) collective-permute-start(s32[1,28]{1,0:T(1,128)S(1)} %copy-done.17), channel_id=1, source_target_pairs={{0,64},{16,80},{32,96},{48,112},{64,0},{80,16},{96,32},{112,48},{1... | collective-permute-start | bytes 344 | tf_op jit(solution)/shard_map/ppermute | solution.py:305
  25.3 15.5 %collective-permute-start.3 = (s32[16]{0:T(128)S(1)}, s32[16]{0:T(128)S(1)}, u32[]{:S(2)}, u32[]{:S(2)}) collective-permute-start(s32[16]{0:T(128)S(1)} %copy-done.18), channel_id=1, source_target_pairs={{0,8},{8,0},{1,9},{9,1},{2,10},{10,2},{3,11},{11,3},{4,12},{12,4},... | collective-permute-start | bytes 200 | tf_op jit(solution)/shard_map/ppermute | solution.py:312
  38.4 23.5 %collective-permute-start.21 = (bf16[112,2560]{1,0:T(8,128)(2,1)S(1)}, bf16[112,2560]{1,0:T(8,128)(2,1)S(1)}, u32[]{:S(2)}, u32[]{:S(2)}) collective-permute-start(bf16[112,2560]{1,0:T(8,128)(2,1)S(1)} %copy-done.7), channel_id=1, source_target_pairs={{0,48},{16,0},{32,16},{48,32},{64,112},{80,64},{96,80},{112,96},{1... | collective-permute-start | bytes 1720328 | tf_op jit(solution)/shard_map/ppermute | solution.py:305
  40.8 4.9 %collective-permute-start.1 = (s32[2,28]{1,0:T(2,128)S(1)}, s32[2,28]{1,0:T(2,128)S(1)}, u32[]{:S(2)}, u32[]{:S(2)}) collective-permute-start(s32[2,28]{1,0:T(2,128)S(1)} %pad_add_fusion.2), channel_id=1, source_target_pairs={{0,16},{16,32},{32,48},{48,0},{64,80},{80,96},{96,112},{112,64},{1... | collective-permute-start | bytes 680 | tf_op jit(solution)/shard_map/ppermute | solution.py:305
  45.6 7.1 %collective-permute-start.2 = (s32[2,28]{1,0:T(2,128)S(1)}, s32[2,28]{1,0:T(2,128)S(1)}, u32[]{:S(2)}, u32[]{:S(2)}) collective-permute-start(s32[2,28]{1,0:T(2,128)S(1)} %pad_add_fusion.2), channel_id=1, source_target_pairs={{0,48},{16,0},{32,16},{48,32},{64,112},{80,64},{96,80},{112,96},{1... | collective-permute-start | bytes 680 | tf_op jit(solution)/shard_map/ppermute | solution.py:305
  52.8 5.2 %collective-permute-start.4 = (s32[2,28]{1,0:T(2,128)S(1)}, s32[2,28]{1,0:T(2,128)S(1)}, u32[]{:S(2)}, u32[]{:S(2)}) collective-permute-start(s32[2,28]{1,0:T(2,128)S(1)} %collective-permute-done.1), channel_id=1, source_target_pairs={{0,16},{16,32},{32,48},{48,0},{64,80},{80,96},{96,112},{112,64},{1... | collective-permute-start | bytes 680 | tf_op jit(solution)/shard_map/ppermute | solution.py:305
  58.0 14.5 %collective-permute-start.22 = (bf16[128,2560]{1,0:T(8,128)(2,1)S(1)}, bf16[128,2560]{1,0:T(8,128)(2,1)}, u32[]{:S(2)}, u32[]{:S(2)}) collective-permute-start(bf16[128,2560]{1,0:T(8,128)(2,1)S(1)} %copy-done.3), channel_id=1, source_target_pairs={{0,48},{16,0},{32,16},{48,32},{64,112},{80,64},{96,80},{112,96},{1... | collective-permute-start | bytes 1966088 | tf_op jit(solution)/shard_map/ppermute | solution.py:305
  60.2 31.0 %collective-permute-start.5 = (bf16[144,2560]{1,0:T(8,128)(2,1)S(1)}, bf16[144,2560]{1,0:T(8,128)(2,1)S(1)}, u32[]{:S(2)}, u32[]{:S(2)}) collective-permute-start(bf16[144,2560]{1,0:T(8,128)(2,1)S(1)} %copy-done.5), channel_id=1, source_target_pairs={{0,16},{16,32},{32,48},{48,0},{64,80},{80,96},{96,112},{112,64},{1... | collective-permute-start | bytes 2211848 | tf_op jit(solution)/shard_map/ppermute | solution.py:305
  60.3 16.3 %collective-permute-start.11 = (bf16[128,2560]{1,0:T(8,128)(2,1)S(1)}, bf16[128,2560]{1,0:T(8,128)(2,1)}, u32[]{:S(2)}, u32[]{:S(2)}) collective-permute-start(bf16[128,2560]{1,0:T(8,128)(2,1)S(1)} %copy-done.3), channel_id=1, source_target_pairs={{0,64},{16,80},{32,96},{48,112},{64,0},{80,16},{96,32},{112,48},{1... | collective-permute-start | bytes 1966088 | tf_op jit(solution)/shard_map/ppermute | solution.py:305
  61.9 0.8 copy-start.15
  61.9 29.3 %collective-permute-start.19 = (bf16[128,2560]{1,0:T(8,128)(2,1)S(1)}, bf16[128,2560]{1,0:T(8,128)(2,1)}, u32[]{:S(2)}, u32[]{:S(2)}) collective-permute-start(bf16[128,2560]{1,0:T(8,128)(2,1)S(1)} %copy-done.3), channel_id=1, source_target_pairs={{0,16},{16,32},{32,48},{48,0},{64,80},{80,96},{96,112},{112,64},{1... | collective-permute-start | bytes 1966088 | tf_op jit(solution)/shard_map/ppermute | solution.py:305
  72.4 22.5 %collective-permute-start.18 = (bf16[144,2560]{1,0:T(8,128)(2,1)S(1)}, bf16[144,2560]{1,0:T(8,128)(2,1)S(1)}, u32[]{:S(2)}, u32[]{:S(2)}) collective-permute-start(bf16[144,2560]{1,0:T(8,128)(2,1)S(1)} %copy-done.5), channel_id=1, source_target_pairs={{0,64},{16,80},{32,96},{48,112},{64,0},{80,16},{96,32},{112,48},{1... | collective-permute-start | bytes 2211848 | tf_op jit(solution)/shard_map/ppermute | solution.py:305
  76.6 18.8 %collective-permute-start.20 = (bf16[144,2560]{1,0:T(8,128)(2,1)S(1)}, bf16[144,2560]{1,0:T(8,128)(2,1)}, u32[]{:S(2)}, u32[]{:S(2)}) collective-permute-start(bf16[144,2560]{1,0:T(8,128)(2,1)S(1)} %copy-done.5), channel_id=1, source_target_pairs={{0,48},{16,0},{32,16},{48,32},{64,112},{80,64},{96,80},{112,96},{1... | collective-permute-start | bytes 2211848 | tf_op jit(solution)/shard_map/ppermute | solution.py:305
  91.2 13.4 %collective-permute-start.28 = (bf16[112,2560]{1,0:T(8,128)(2,1)}, bf16[112,2560]{1,0:T(8,128)(2,1)S(1)}, u32[]{:S(2)}, u32[]{:S(2)}) collective-permute-start(bf16[112,2560]{1,0:T(8,128)(2,1)} %collective-permute-done.15.refs_8_), channel_id=1, source_target_pairs={{0,16},{16,32},{32,48},{48,0},{64,80},{80,96},{96,112},{112,64},{1... | collective-permute-start | bytes 1720328 | tf_op jit(solution)/shard_map/ppermute | solution.py:305
  91.2 50.0 %copy-start.10 = (bf16[144,2560]{1,0:T(8,128)(2,1)}, bf16[144,2560]{1,0:T(8,128)(2,1)S(1)}, u32[]{:S(2)}) copy-start(bf16[144,2560]{1,0:T(8,128)(2,1)S(1)} %collective-permute-done.5.refs_7_) | copy-start | bytes 2211844
  91.2 16.9 %collective-permute-start.9 = (bf16[112,2560]{1,0:T(8,128)(2,1)}, bf16[112,2560]{1,0:T(8,128)(2,1)}, u32[]{:S(2)}, u32[]{:S(2)}) collective-permute-start(bf16[112,2560]{1,0:T(8,128)(2,1)} %collective-permute-done.8.refs_5_), channel_id=1, source_target_pairs={{0,48},{16,0},{32,16},{48,32},{64,112},{80,64},{96,80},{112,96},{1... | collective-permute-start | bytes 1720328 | tf_op jit(solution)/shard_map/ppermute | solution.py:305
  95.0 46.2 %copy-start.11 = (bf16[144,2560]{1,0:T(8,128)(2,1)}, bf16[144,2560]{1,0:T(8,128)(2,1)S(1)}, u32[]{:S(2)}) copy-start(bf16[144,2560]{1,0:T(8,128)(2,1)S(1)} %collective-permute-done.18.refs_4_) | copy-start | bytes 2211844
  95.0 27.2 %collective-permute-start.29 = (bf16[128,2560]{1,0:T(8,128)(2,1)}, bf16[128,2560]{1,0:T(8,128)(2,1)}, u32[]{:S(2)}, u32[]{:S(2)}) collective-permute-start(bf16[128,2560]{1,0:T(8,128)(2,1)} %collective-permute-done.22.refs_12_), channel_id=1, source_target_pairs={{0,48},{16,0},{32,16},{48,32},{64,112},{80,64},{96,80},{112,96},{1... | collective-permute-start | bytes 1966088 | tf_op jit(solution)/shard_map/ppermute | solution.py:305
  95.2 46.0 %copy-start.20 = (s32[48]{0:T(128)}, s32[48]{0:T(128)S(1)}, u32[]{:S(2)}) copy-start(s32[48]{0:T(128)S(1)} %reshape.93.refs_0_) | copy-start | bytes 580
  95.4 27.7 %collective-permute-start.31 = (bf16[128,2560]{1,0:T(8,128)(2,1)}, bf16[128,2560]{1,0:T(8,128)(2,1)}, u32[]{:S(2)}, u32[]{:S(2)}) collective-permute-start(bf16[128,2560]{1,0:T(8,128)(2,1)} %collective-permute-done.22.refs_12_), channel_id=1, source_target_pairs={{0,64},{16,80},{32,96},{48,112},{64,0},{80,16},{96,32},{112,48},{1... | collective-permute-start | bytes 1966088 | tf_op jit(solution)/shard_map/ppermute | solution.py:305
  104.6 0.8 copy-start.16
  104.6 33.5 %collective-permute-start.6 = (bf16[144,2560]{1,0:T(8,128)(2,1)S(1)}, bf16[144,2560]{1,0:T(8,128)(2,1)S(1)}, u32[]{:S(2)}, u32[]{:S(2)}) collective-permute-start(bf16[144,2560]{1,0:T(8,128)(2,1)S(1)} %collective-permute-done.5.refs_7_), channel_id=1, source_target_pairs={{0,16},{16,32},{32,48},{48,0},{64,80},{80,96},{96,112},{112,64},{1... | collective-permute-start | bytes 2211848 | tf_op jit(solution)/shard_map/ppermute | solution.py:305
  108.1 32.2 %collective-permute-start.30 = (bf16[144,2560]{1,0:T(8,128)(2,1)S(1)}, bf16[144,2560]{1,0:T(8,128)(2,1)S(1)}, u32[]{:S(2)}, u32[]{:S(2)}) collective-permute-start(bf16[144,2560]{1,0:T(8,128)(2,1)S(1)} %collective-permute-done.18.refs_4_), channel_id=1, source_target_pairs={{0,48},{16,0},{32,16},{48,32},{64,112},{80,64},{96,80},{112,96},{1... | collective-permute-start | bytes 2211848 | tf_op jit(solution)/shard_map/ppermute | solution.py:305
  122.2 14.4 %collective-permute-start.12 = (bf16[128,2560]{1,0:T(8,128)(2,1)}, bf16[128,2560]{1,0:T(8,128)(2,1)}, u32[]{:S(2)}, u32[]{:S(2)}) collective-permute-start(bf16[128,2560]{1,0:T(8,128)(2,1)} %collective-permute-done.11.refs_6_), channel_id=1, source_target_pairs={{0,16},{16,32},{32,48},{48,0},{64,80},{80,96},{96,112},{112,64},{1... | collective-permute-start | bytes 1966088 | tf_op jit(solution)/shard_map/ppermute | solution.py:305
  123.2 37.8 %collective-permute-start.14 = (bf16[144,2560]{1,0:T(8,128)(2,1)S(1)}, bf16[144,2560]{1,0:T(8,128)(2,1)S(1)}, u32[]{:S(2)}, u32[]{:S(2)}) collective-permute-start(bf16[144,2560]{1,0:T(8,128)(2,1)S(1)} %collective-permute-done.5.refs_7_), channel_id=1, source_target_pairs={{0,64},{16,80},{32,96},{48,112},{64,0},{80,16},{96,32},{112,48},{1... | collective-permute-start | bytes 2211848 | tf_op jit(solution)/shard_map/ppermute | solution.py:305
  125.3 25.4 %copy-start.21 = (f32[1,384]{1,0:T(1,128)S(1)}, f32[1,384]{1,0:T(1,128)}, u32[]{:S(2)}) copy-start(f32[1,384]{1,0:T(1,128)} %get-tuple-element.21) | copy-start | bytes 4612
  125.3 26.1 %copy-start.22 = (f32[1,384]{1,0:T(1,128)S(1)}, f32[1,384]{1,0:T(1,128)}, u32[]{:S(2)}) copy-start(f32[1,384]{1,0:T(1,128)} %get-tuple-element.23) | copy-start | bytes 4612
  136.6 21.6 %collective-permute-start.16 = (bf16[112,2560]{1,0:T(8,128)(2,1)}, bf16[112,2560]{1,0:T(8,128)(2,1)S(1)}, u32[]{:S(2)}, u32[]{:S(2)}) collective-permute-start(bf16[112,2560]{1,0:T(8,128)(2,1)} %collective-permute-done.15.refs_8_), channel_id=1, source_target_pairs={{0,64},{16,80},{32,96},{48,112},{64,0},{80,16},{96,32},{112,48},{1... | collective-permute-start | bytes 1720328 | tf_op jit(solution)/shard_map/ppermute | solution.py:305
  138.0 12.6 %copy-start.12 = (bf16[144,2560]{1,0:T(8,128)(2,1)}, bf16[144,2560]{1,0:T(8,128)(2,1)S(1)}, u32[]{:S(2)}) copy-start(bf16[144,2560]{1,0:T(8,128)(2,1)S(1)} %collective-permute-done.6.refs_1_) | copy-start | bytes 2211844
  138.0 27.2 %collective-permute-start.10 = (bf16[112,2560]{1,0:T(8,128)(2,1)}, bf16[112,2560]{1,0:T(8,128)(2,1)S(1)}, u32[]{:S(2)}, u32[]{:S(2)}) collective-permute-start(bf16[112,2560]{1,0:T(8,128)(2,1)} %collective-permute-done.9.refs_5_), channel_id=1, source_target_pairs={{0,48},{16,0},{32,16},{48,32},{64,112},{80,64},{96,80},{112,96},{1... | collective-permute-start | bytes 1720328 | tf_op jit(solution)/shard_map/ppermute | solution.py:305
  140.4 10.3 %copy-start.13 = (bf16[144,2560]{1,0:T(8,128)(2,1)}, bf16[144,2560]{1,0:T(8,128)(2,1)S(1)}, u32[]{:S(2)}) copy-start(bf16[144,2560]{1,0:T(8,128)(2,1)S(1)} %collective-permute-done.30.refs_4_) | copy-start | bytes 2211844
  140.4 31.1 %collective-permute-start.13 = (bf16[128,2560]{1,0:T(8,128)(2,1)}, bf16[128,2560]{1,0:T(8,128)(2,1)S(1)}, u32[]{:S(2)}, u32[]{:S(2)}) collective-permute-start(bf16[128,2560]{1,0:T(8,128)(2,1)} %collective-permute-done.12.refs_3_), channel_id=1, source_target_pairs={{0,16},{16,32},{32,48},{48,0},{64,80},{80,96},{96,112},{112,64},{1... | collective-permute-start | bytes 1966088 | tf_op jit(solution)/shard_map/ppermute | solution.py:305
  140.4 34.1 %collective-permute-start.7 = (bf16[144,2560]{1,0:T(8,128)(2,1)S(1)}, bf16[144,2560]{1,0:T(8,128)(2,1)S(1)}, u32[]{:S(2)}, u32[]{:S(2)}) collective-permute-start(bf16[144,2560]{1,0:T(8,128)(2,1)S(1)} %collective-permute-done.6.refs_1_), channel_id=1, source_target_pairs={{0,64},{16,80},{32,96},{48,112},{64,0},{80,16},{96,32},{112,48},{1... | collective-permute-start | bytes 2211848 | tf_op jit(solution)/shard_map/ppermute | solution.py:305
  158.2 7.1 %copy-start.14 = (bf16[112,2560]{1,0:T(8,128)(2,1)}, bf16[112,2560]{1,0:T(8,128)(2,1)S(1)}, u32[]{:S(2)}) copy-start(bf16[112,2560]{1,0:T(8,128)(2,1)S(1)} %collective-permute-done.16.refs_2_) | copy-start | bytes 1720324
  158.2 16.3 %collective-permute-start.32 = (f32[1,384]{1,0:T(1,128)}, f32[1,384]{1,0:T(1,128)S(1)}, u32[]{:S(2)}, u32[]{:S(2)}) collective-permute-start(f32[1,384]{1,0:T(1,128)} %get-tuple-element.28), channel_id=1, source_target_pairs={{0,64},{16,80},{32,96},{48,112},{64,0},{80,16},{96,32},{112,48},{1... | collective-permute-start | bytes 4616 | tf_op jit(solution)/shard_map/ppermute | solution.py:305
  161.0 4.3 %copy-start.9 = (bf16[144,2560]{1,0:T(8,128)(2,1)}, bf16[144,2560]{1,0:T(8,128)(2,1)S(1)}, u32[]{:S(2)}) copy-start(bf16[144,2560]{1,0:T(8,128)(2,1)S(1)} %collective-permute-done.14.refs_1_) | copy-start | bytes 2211844
  161.0 10.5 %copy-start.25 = (f32[1,384]{1,0:T(1,128)S(1)}, f32[1,384]{1,0:T(1,128)}, u32[]{:S(2)}) copy-start(f32[1,384]{1,0:T(1,128)} %get-tuple-element.24) | copy-start | bytes 4612
  161.0 13.5 %copy-start.24 = (f32[1,384]{1,0:T(1,128)S(1)}, f32[1,384]{1,0:T(1,128)}, u32[]{:S(2)}) copy-start(f32[1,384]{1,0:T(1,128)} %get-tuple-element.25) | copy-start | bytes 4612
  161.0 13.6 %copy-start.23 = (f32[1,384]{1,0:T(1,128)S(1)}, f32[1,384]{1,0:T(1,128)}, u32[]{:S(2)}) copy-start(f32[1,384]{1,0:T(1,128)} %get-tuple-element.26) | copy-start | bytes 4612
  161.0 22.7 %copy-start.8 = (s32[64]{0:T(128)S(1)}, s32[64]{0:T(128)}, u32[]{:S(2)}) copy-start(s32[64]{0:T(128)} %pad_add_fusion.8.refs_0_) | copy-start | bytes 772
  161.0 17.7 %collective-permute-start.33 = (f32[1,384]{1,0:T(1,128)}, f32[1,384]{1,0:T(1,128)S(1)}, u32[]{:S(2)}, u32[]{:S(2)}) collective-permute-start(f32[1,384]{1,0:T(1,128)} %get-tuple-element.29), channel_id=1, source_target_pairs={{0,48},{16,0},{32,16},{48,32},{64,112},{80,64},{96,80},{112,96},{1... | collective-permute-start | bytes 4616 | tf_op jit(solution)/shard_map/ppermute | solution.py:305
  165.3 18.4 %collective-permute-start.23 = (f32[3,384]{1,0:T(4,128)S(1)}, f32[3,384]{1,0:T(4,128)S(1)}, u32[]{:S(2)}, u32[]{:S(2)}) collective-permute-start(f32[3,384]{1,0:T(4,128)S(1)} %pad_maximum_fusion), channel_id=1, source_target_pairs={{0,96},{16,112},{32,64},{48,80},{64,32},{80,48},{96,0},{112,16},{1... | collective-permute-start | bytes 13832 | tf_op jit(solution)/shard_map/ppermute | solution.py:305
  171.4 7.2 %collective-permute-start.24 = (f32[1,384]{1,0:T(1,128)S(1)}, f32[1,384]{1,0:T(1,128)S(1)}, u32[]{:S(2)}, u32[]{:S(2)}) collective-permute-start(f32[1,384]{1,0:T(1,128)S(1)} %copy-done.25), channel_id=1, source_target_pairs={{0,32},{16,48},{32,0},{48,16},{64,96},{80,112},{96,64},{112,80},{1... | collective-permute-start | bytes 4616 | tf_op jit(solution)/shard_map/ppermute | solution.py:305
  174.5 5.7 %collective-permute-start.25 = (f32[1,384]{1,0:T(1,128)S(1)}, f32[1,384]{1,0:T(1,128)S(1)}, u32[]{:S(2)}, u32[]{:S(2)}) collective-permute-start(f32[1,384]{1,0:T(1,128)S(1)} %copy-done.24), channel_id=1, source_target_pairs={{0,80},{16,96},{32,112},{48,64},{64,16},{80,32},{96,48},{112,0},{1... | collective-permute-start | bytes 4616 | tf_op jit(solution)/shard_map/ppermute | solution.py:305
  174.5 5.7 %collective-permute-start.26 = (f32[1,384]{1,0:T(1,128)S(1)}, f32[1,384]{1,0:T(1,128)S(1)}, u32[]{:S(2)}, u32[]{:S(2)}) collective-permute-start(f32[1,384]{1,0:T(1,128)S(1)} %copy-done.23), channel_id=1, source_target_pairs={{0,112},{16,64},{32,80},{48,96},{64,48},{80,0},{96,16},{112,32},{1... | collective-permute-start | bytes 4616 | tf_op jit(solution)/shard_map/ppermute | solution.py:305
  178.7 5.0 %collective-permute-start.27 = (f32[1,384]{1,0:T(1,128)}, f32[1,384]{1,0:T(1,128)S(1)}, u32[]{:S(2)}, u32[]{:S(2)}) collective-permute-start(f32[1,384]{1,0:T(1,128)} %get-tuple-element.27), channel_id=1, source_target_pairs={{0,16},{16,32},{32,48},{48,0},{64,80},{80,96},{96,112},{112,64},{1... | collective-permute-start | bytes 4616 | tf_op jit(solution)/shard_map/ppermute | solution.py:305
  183.7 1.7 copy-start.1
  187.7 21.1 %collective-permute-start.34 = (f32[384]{0:T(512)S(1)}, f32[384]{0:T(512)S(1)}, u32[]{:S(2)}, u32[]{:S(2)}) collective-permute-start(f32[384]{0:T(512)S(1)} %reduce), channel_id=1, source_target_pairs={{0,96},{16,112},{32,64},{48,80},{64,32},{80,48},{96,0},{112,16},{1... | collective-permute-start | bytes 4616 | tf_op jit(solution)/shard_map/ppermute | solution.py:305
